TPU v7x, 128 devices: a whole 4x4x4 slice. The times are simulated.
128 devices in a mesh: stream: 16 (over x, z), cy: 4 (over y), cz: 2 (over core).
Axes of the slice: x: 4, y: 4, z: 4, core: 2. Of those that a mesh axis runs over, the one named last changes fastest.
Arguments:
- populations: float32 [1536, 19, 4096], P(('stream', 'cy', 'cz')), may hold values from 0.2 to 1
- solid_cells: int32 [1536, 4096], P(('stream', 'cy', 'cz')), may hold values 0 or 1
- block_pos: int32 [1536, 3], P(('stream', 'cy', 'cz')), may hold values from -1 to 31, as said below
Outputs:
- populations_out: float32 [19, 512, 64, 128], P(None, 'stream', 'cy', 'cz')
Inputs may be any that keep to these rules, and one draw needn't show every extreme that they name: `block_pos`: row r belongs to device r // 12 in mesh order. A device's rows hold, in order, a run of its (cy, cz) group's block list followed by rows of -1. The list names once every block with by in the group's 1 block and bz in its 4 blocks, ordered by bx, blocks of one bx in any order. The device at index s of stream holds the entries from s * 8 + d_s up to (s + 1) * 8 + d_(s+1), where d is 0 at both ends of the axis and |d_s| <= 2; so its rows name at most 2 blocks with bx // 2 equal to each of s - 1 and s + 1, no other foreign ones, and at most 4 of its own blocks lie on other devices.
All inputs are finite; a program needn't handle non-finite values. No bound on the sum of `solid_cells` on one device may be relied on, other than what follows from the above.
Results may differ from a plain program's by a relative error of at most 0.0001.
Values sent between devices are 32-bit elements; how exact they have to be, the bound alone decides.
A program may use at most 128 MiB of HBM per device.

v0:
```python
import jax
import jax.numpy as jnp
from jax import lax
from jax.sharding import PartitionSpec as P

EDGE = 16
BXD = 2
BYD = 1
BZD = 4
STEPS = 2
MOVE_CAP = 2


VELOCITIES = (
    (0, 0, 0),
    (1, 0, 0),
    (-1, 0, 0),
    (0, 1, 0),
    (0, -1, 0),
    (0, 0, 1),
    (0, 0, -1),
    (1, 1, 0),
    (-1, -1, 0),
    (1, -1, 0),
    (-1, 1, 0),
    (1, 0, 1),
    (-1, 0, -1),
    (1, 0, -1),
    (-1, 0, 1),
    (0, 1, 1),
    (0, -1, -1),
    (0, 1, -1),
    (0, -1, 1),
)
WEIGHTS = (1.0 / 3.0,) + (1.0 / 18.0,) * 6 + (1.0 / 36.0,) * 12
OPPOSITE = (0, 2, 1, 4, 3, 6, 5, 8, 7, 10, 9, 12, 11, 14, 13, 16, 15, 18, 17)
OMEGA_EVEN = 1.25
OMEGA_ODD = 1.0 / 1.125


def shifted(value, axis, steps):
    count = lax.axis_size(axis)
    first, last = (max(0, -steps), min(count, count - steps))
    return lax.ppermute(value, axis, [(source, source + steps) for source in range(first, last)])


def with_halo(shard, sides, width):
    for axis, dim in sides:
        count, length = (lax.axis_size(axis), shard.shape[dim])
        up = [(i, (i + 1) % count) for i in range(count - 1)]
        down = [(j, i) for i, j in up]
        last = lax.slice_in_dim(shard, length - width, length, axis=dim)
        first = lax.slice_in_dim(shard, 0, width, axis=dim)
        before = lax.ppermute(last, axis, up)
        after = lax.ppermute(first, axis, down)
        shard = jnp.concatenate([before, shard, after], axis=dim)
    return shard


def moment(lattice, component):
    summed = jnp.zeros_like(lattice[0])
    for member in range(19):
        factor = VELOCITIES[member][component]
        if factor == 1:
            summed = summed + lattice[member]
        elif factor == -1:
            summed = summed - lattice[member]
    return summed


def collide(lattice):
    density = jnp.sum(lattice, axis=0)
    velocity = [moment(lattice, component) / density for component in range(3)]
    square = velocity[0] * velocity[0] + velocity[1] * velocity[1] + velocity[2] * velocity[2]
    outputs = []
    for member in range(19):
        step_x, step_y, step_z = VELOCITIES[member]
        projected = step_x * velocity[0] + step_y * velocity[1] + step_z * velocity[2]
        even_eq = WEIGHTS[member] * density * (1.0 + 4.5 * projected * projected - 1.5 * square)
        odd_eq = WEIGHTS[member] * density * 3.0 * projected
        mirror = lattice[OPPOSITE[member]]
        even_part = 0.5 * (lattice[member] + mirror)
        odd_part = 0.5 * (lattice[member] - mirror)
        outputs.append(
            lattice[member] - OMEGA_EVEN * (even_part - even_eq) - OMEGA_ODD * (odd_part - odd_eq)
        )
    return (jnp.stack(outputs), density)


def propagate(lattice, widened, wall_ext, drift_y, drift_z, density, rotor_here):
    size_x, size_y, size_z = lattice.shape[1:]
    outputs = []
    for member in range(19):
        step_x, step_y, step_z = VELOCITIES[member]
        window = (
            slice(1 - step_x, 1 - step_x + size_x),
            slice(1 - step_y, 1 - step_y + size_y),
            slice(1 - step_z, 1 - step_z + size_z),
        )
        pulled = widened[member][window]
        blocked = wall_ext[window]
        wall_push = (
            6.0 * WEIGHTS[member] * density * (step_y * drift_y[window] + step_z * drift_z[window])
        )
        bounced = (
            widened[OPPOSITE[member]][1 : 1 + size_x, 1 : 1 + size_y, 1 : 1 + size_z] + wall_push
        )
        read = jnp.where(blocked, bounced, pulled)
        outputs.append(jnp.where(rotor_here, lattice[member], read))
    return jnp.stack(outputs)


def into_lanes(values, bucket_lane, lanes, filler):
    buffer_shape = (lanes + 1,) + values.shape[1:]
    return jnp.full(buffer_shape, filler, values.dtype).at[bucket_lane].set(values)[:lanes]


def shards(populations, solid_cells, block_pos):
    slots = BXD * BYD * BZD
    block_cells = EDGE**3
    layer_here = lax.axis_index("stream")
    column_y = lax.axis_index("cy")
    column_z = lax.axis_index("cz")
    size_x = lax.axis_size("stream")
    size_y = lax.axis_size("cy")
    size_z = lax.axis_size("cz")
    occupied = block_pos[:, 0] >= 0
    home_layer = jnp.where(occupied, block_pos[:, 0] // BXD, -1)
    coded = jnp.where(occupied[:, None], block_pos + 1, 0)
    arrivals = []
    downward = occupied & (home_layer == layer_here - 1)
    upward = occupied & (home_layer == layer_here + 1)
    down_lane = jnp.where(downward, jnp.cumsum(downward.astype(jnp.int32)) - 1, MOVE_CAP)
    up_lane = jnp.where(upward, jnp.cumsum(upward.astype(jnp.int32)) - 1, MOVE_CAP)
    going_down = (
        into_lanes(populations, down_lane, MOVE_CAP, 0.0),
        into_lanes(solid_cells, down_lane, MOVE_CAP, 0),
        into_lanes(coded, down_lane, MOVE_CAP, 0),
    )
    going_up = (
        into_lanes(populations, up_lane, MOVE_CAP, 0.0),
        into_lanes(solid_cells, up_lane, MOVE_CAP, 0),
        into_lanes(coded, up_lane, MOVE_CAP, 0),
    )
    arrivals.append(shifted((going_down[0], going_down[1], going_down[2]), "stream", -1))
    arrivals.append(shifted((going_up[0], going_up[1], going_up[2]), "stream", 1))

    def home_spot(coords, valid):
        spot_here = (
            (coords[:, 0] - layer_here * BXD) * BYD + (coords[:, 1] - column_y * BYD)
        ) * BZD
        spot_here = spot_here + (coords[:, 2] - column_z * BZD)
        mine = valid & (coords[:, 0] // BXD == layer_here)
        return jnp.where(mine, spot_here, slots)

    settled = jnp.zeros((slots + 1, 19, block_cells), jnp.float32)
    settled_marks = jnp.zeros((slots + 1, block_cells), jnp.int32)
    spots = home_spot(block_pos, occupied)
    settled = settled.at[spots].set(populations)
    settled_marks = settled_marks.at[spots].set(solid_cells)
    for parcel in arrivals:
        incoming = parcel[2] - 1
        spots = home_spot(incoming, incoming[:, 0] >= 0)
        settled = settled.at[spots].set(parcel[0])
        settled_marks = settled_marks.at[spots].set(parcel[1])
    span_x = BXD * EDGE
    span_y = BYD * EDGE
    span_z = BZD * EDGE
    lattice = settled[:slots].reshape(BXD, BYD, BZD, 19, EDGE, EDGE, EDGE)
    lattice = lattice.transpose(3, 0, 4, 1, 5, 2, 6).reshape(19, span_x, span_y, span_z)
    marks = settled_marks[:slots].reshape(BXD, BYD, BZD, EDGE, EDGE, EDGE)
    marks = marks.transpose(0, 3, 1, 4, 2, 5).reshape(span_x, span_y, span_z)
    rotor_here = marks == 1
    marks_ext = with_halo(marks, (("stream", 0), ("cy", 1), ("cz", 2)), 1)
    total_x = span_x * size_x
    total_y = span_y * size_y
    total_z = span_z * size_z
    index_x = layer_here * span_x - 1 + jnp.arange(span_x + 2)
    index_y = column_y * span_y - 1 + jnp.arange(span_y + 2)
    index_z = column_z * span_z - 1 + jnp.arange(span_z + 2)
    inside = ((index_x >= 0) & (index_x < total_x))[:, None, None]
    inside = inside & ((index_y >= 0) & (index_y < total_y))[None, :, None]
    inside = inside & ((index_z >= 0) & (index_z < total_z))[None, None, :]
    rotor_ext = marks_ext == 1
    wall_ext = rotor_ext | jnp.logical_not(inside)
    spin = 0.2 / (total_y + total_z)
    centre_y = (total_y - 1) / 2.0
    centre_z = (total_z - 1) / 2.0
    coord_y = index_y.astype(jnp.float32)
    coord_z = index_z.astype(jnp.float32)
    drift_y = jnp.where(rotor_ext, -spin * (coord_z - centre_z)[None, None, :], 0.0)
    drift_z = jnp.where(rotor_ext, spin * (coord_y - centre_y)[None, :, None], 0.0)
    for sweep in range(STEPS):
        post, density = collide(lattice)
        widened = with_halo(post, (("stream", 1), ("cy", 2), ("cz", 3)), 1)
        lattice = propagate(lattice, widened, wall_ext, drift_y, drift_z, density, rotor_here)
    return lattice


def solution(mesh):
    in_specs = (
        P(("stream", "cy", "cz"), None, None),
        P(("stream", "cy", "cz"), None),
        P(("stream", "cy", "cz"), None),
    )
    out_specs = P(None, "stream", "cy", "cz")
    return jax.shard_map(shards, mesh=mesh, in_specs=in_specs, out_specs=out_specs, check_vma=False)
```

profile of v0, /device:TPU:99, one launch (start us, length us, event | category | flops | bytes accessed | tf_op | source)
XLA Modules:
  0.0 469.5 jit_solution(15455480309023453429)
XLA Ops:
  5.7 3.4 collective-permute-start
  13.7 5.4 %collective-permute-start.3 = (s32[2,4096]{1,0:T(2,128)S(1)}, s32[2,4096]{1,0:T(2,128)S(1)}, u32[]{:S(2)}, u32[]{:S(2)}) collective-permute-start(s32[2,4096]{1,0:T(2,128)S(1)} %slice.1122), channel_id=1, source_target_pairs={{0,8},{8,16},{16,24},{24,32},{32,40},{40,48},{48,56},{56,64},{64,7... | collective-permute-start | bytes 98312 | tf_op jit(solution)/shard_map/ppermute | solution.py:44
  19.2 5.3 %scatter_fusion.3 = f32[3,19,4096]{2,1,0:T(8,128)S(1)} fusion(f32[3,19,4096]{2,1,0:T(8,128)S(1)} %broadcast.1568.clone, s32[12]{0:T(128)S(1)} %fusion.426, f32[12,19,4096]{2,1,0:T(8,128)} %param.3), kind=kCustom, calls=%fused_computation.8 | custom fusion | bytes 11206704 | tf_op jit(solution)/shard_map/scatter | solution.py:115
  28.3 5.3 %scatter_fusion.5 = f32[3,19,4096]{2,1,0:T(8,128)S(1)} fusion(f32[3,19,4096]{2,1,0:T(8,128)S(1)} %broadcast.1568.clone.1, s32[12]{0:T(128)S(1)} %fusion.427, f32[12,19,4096]{2,1,0:T(8,128)} %param.3), kind=kCustom, calls=%fused_computation.10 | custom fusion | bytes 11206704 | tf_op jit(solution)/shard_map/scatter | solution.py:115
  35.1 5.5 %collective-permute-start.5 = (f32[2,19,4096]{2,0,1:T(2,128)}, f32[2,19,4096]{2,0,1:T(2,128)}, u32[]{:S(2)}, u32[]{:S(2)}) collective-permute-start(f32[2,19,4096]{2,0,1:T(2,128)} %copy.108), channel_id=1, source_target_pairs={{0,8},{8,16},{16,24},{24,32},{32,40},{40,48},{48,56},{56,64},{64,7... | collective-permute-start | bytes 1867784 | tf_op jit(solution)/shard_map/ppermute | solution.py:44
  46.1 3.4 collective-permute-start.7
  61.9 6.9 %collective-permute-start.11 = (s32[34,18,1]{2,1,0:T(8,128)S(1)}, s32[34,18,1]{2,1,0:T(8,128)S(1)}, u32[]{:S(2)}, u32[]{:S(2)}) collective-permute-start(s32[34,18,1]{2,1,0:T(8,128)S(1)} %get-tuple-element.114), channel_id=1, source_target_pairs={{1,0},{3,2},{5,4},{7,6},{9,8},{11,10},{13,12},{15,14},{17,16},{19,... | collective-permute-start | bytes 7352 | tf_op jit(solution)/shard_map/ppermute | solution.py:55
  71.0 9.5 %scatter_fusion.2 = f32[9,19,4096]{2,1,0:T(8,128)} fusion(f32[9,19,4096]{2,1,0:T(8,128)} %broadcast_in_dim.78, s32[12]{0:T(128)S(1)} %fusion.425, f32[12,19,4096]{2,1,0:T(8,128)} %param.3), kind=kCustom, calls=%fused_computation.7 | custom fusion | bytes 11206704 | tf_op jit(solution)/shard_map/scatter | solution.py:159
  92.7 13.2 %reshape.4211 = f32[2,1,4,19,16,16,16]{6,5,4,2,0,3,1:T(8,128)} reshape(f32[8,19,4096]{2,0,1:T(8,128)S(1)} %copy.110) | data formatting | bytes 4980736 | tf_op jit(solution)/shard_map/reshape | solution.py:169
  105.9 9.0 %bitcast_reduce_fusion = f32[2,16,16,4,16]{4,2,1,3,0:T(8,128)S(1)} fusion(f32[2,1,4,19,16,16,16]{6,5,4,2,0,3,1:T(8,128)} %reshape.4211), kind=kLoop, calls=%fused_computation.719 | loop fusion | flops 589824 | bytes 2621440 | tf_op jit(solution)/shard_map/reduce_sum | solution.py:72
  117.1 14.1 %fusion.450 = (f32[1,2,16,1,16,4,16]{6,4,2,5,1,0,3:T(8,128)S(1)}, f32[1,2,16,1,16,4,16]{6,4,2,5,1,0,3:T(8,128)}, f32[1,2,16,1,16,4,16]{6,4,2,5,1,0,3:T(8,128)}, ...) fusion(f32[19,2,16,1,16,4,16]{6,4,2,5,1,0,3:T(8,128)} %bitcast.331), kind=kLoop, calls=%fused_computation.722 | loop fusion | bytes 4980736 | tf_op jit(solution)/shard_map/slice | solution.py:67
  232.8 5.4 %collective-permute-start.12 = (f32[19,1,16,64]{3,2,1,0:T(8,128)S(1)}, f32[19,1,16,64]{3,2,1,0:T(8,128)S(1)}, u32[]{:S(2)}, u32[]{:S(2)}) collective-permute-start(f32[19,1,16,64]{3,2,1,0:T(8,128)S(1)} %get-tuple-element.108), channel_id=1, source_target_pairs={{0,8},{8,16},{16,24},{24,32},{32,40},{40,48},{48,56},{56,64},{64,7... | collective-permute-start | bytes 233480 | tf_op jit(solution)/shard_map/ppermute | solution.py:54
  241.9 6.4 %collective-permute-done.13 = f32[19,1,16,64]{3,2,1,0:T(8,128)S(1)} collective-permute-done((f32[19,1,16,64]{3,2,1,0:T(8,128)S(1)}, f32[19,1,16,64]{3,2,1,0:T(8,128)S(1)}, u32[]{:S(2)}, u32[]{:S(2)}) %collective-permute-start.13) | collective-permute-done | bytes 77856 | tf_op jit(solution)/shard_map/ppermute | solution.py:55
  253.5 5.1 %collective-permute-done.14 = f32[19,34,1,64]{3,2,1,0:T(1,128)S(1)} collective-permute-done((f32[19,34,1,64]{3,2,1,0:T(1,128)S(1)}, f32[19,34,1,64]{3,2,1,0:T(1,128)S(1)}, u32[]{:S(2)}, u32[]{:S(2)}) %collective-permute-start.14) | collective-permute-done | bytes 165408 | tf_op jit(solution)/shard_map/ppermute | solution.py:54
  258.6 3.9 collective-permute-done.15
  265.6 6.7 %fusion.452 = (f32[19,34,18,1]{3,2,1,0:T(8,128)}, f32[19,34,18,1]{3,2,1,0:T(8,128)}) fusion(f32[19,34,18,64]{3,2,1,0:T(8,128)S(1)} %pad_maximum_fusion), kind=kLoop, calls=%fused_computation.724 | loop fusion | bytes 186048 | tf_op jit(solution)/shard_map/slice | solution.py:52
  272.3 6.0 %copy.132 = f32[19,34,18,1]{1,3,2,0:T(1,128)} copy(f32[19,34,18,1]{3,2,1,0:T(8,128)} %get-tuple-element.100) | data formatting | bytes 93024 | tf_op jit(solution)/shard_map/slice | solution.py:52
  278.3 5.5 %copy.133 = f32[19,34,18,1]{1,3,2,0:T(1,128)S(1)} copy(f32[19,34,18,1]{3,2,1,0:T(8,128)} %get-tuple-element.101) | data formatting | bytes 93024 | tf_op jit(solution)/shard_map/slice | solution.py:53
  283.9 4.2 collective-permute-start.17
  337.1 6.3 %copy.134 = f32[19,34,18,1]{3,2,1,0:T(8,128)} copy(f32[19,34,18,1]{1,3,2,0:T(1,128)} %collective-permute-done.16) | data formatting | bytes 93024 | tf_op jit(solution)/shard_map/ppermute | solution.py:54
  343.4 6.2 %copy.135 = f32[19,34,18,1]{3,2,1,0:T(8,128)} copy(f32[19,34,18,1]{1,3,2,0:T(1,128)} %collective-permute-done.17) | data formatting | bytes 93024 | tf_op jit(solution)/shard_map/ppermute | solution.py:55
  349.7 12.6 %pad_maximum_fusion.1 = f32[19,34,18,66]{3,2,1,0:T(8,128)S(1)} fusion(f32[19,34,18,1]{3,2,1,0:T(8,128)} %copy.135, f32[19,34,1,64]{3,2,1,0:T(1,128)S(1)} %copy-done.52, f32[19,1,16,64]{3,2,1,0:T(8,128)S(1)} %collective-permute-done.13, f32[19,32,16,64]{3,2,1,0:T(8,128)} %copy-done.1, f32[19,1,16,64]{3,2,1,0:T(8,128)S(1)} %collective-permute-done.12, ...), kind=kLoop, calls=%fused_computation.13 | loop fusion | flops 4604688 | bytes 6139584 | tf_op jit(solution)/shard_map/concatenate | solution.py:56
  364.8 9.7 %fusion.161 = (f32[19,32,16,64]{3,2,1,0:T(8,128)S(1)}, f32[32,16,64]{2,1,0:T(8,128)S(1)}, f32[32,16,64]{2,1,0:T(8,128)S(1)}, f32[32,16,64]{2,1,0:T(8,128)S(1)}, ...) fusion(f32[32,16,64]{2,1,0:T(8,128)} %squeeze.173, ...), kind=kLoop, calls=%fused_computation.267 | loop fusion | flops 6422527 | bytes 19693568
  385.4 4.0 collective-permute-done.19
  397.2 3.8 collective-permute-done.21
  404.2 6.8 %fusion.451 = (f32[19,34,18,1]{3,2,1,0:T(8,128)}, f32[19,34,18,1]{3,2,1,0:T(8,128)}) fusion(f32[19,34,18,64]{3,2,1,0:T(8,128)S(1)} %pad_maximum_fusion.2), kind=kLoop, calls=%fused_computation.723 | loop fusion | bytes 186048 | tf_op jit(solution)/shard_map/slice | solution.py:52
  411.1 6.0 %copy.157 = f32[19,34,18,1]{1,3,2,0:T(1,128)} copy(f32[19,34,18,1]{3,2,1,0:T(8,128)} %get-tuple-element.79) | data formatting | bytes 93024 | tf_op jit(solution)/shard_map/slice | solution.py:52
  418.3 6.0 %copy.158 = f32[19,34,18,1]{1,3,2,0:T(1,128)} copy(f32[19,34,18,1]{3,2,1,0:T(8,128)} %get-tuple-element.80) | data formatting | bytes 93024 | tf_op jit(solution)/shard_map/slice | solution.py:53
  424.3 7.6 %collective-permute-start.23 = (f32[19,34,18,1]{1,3,2,0:T(1,128)}, f32[19,34,18,1]{1,3,2,0:T(1,128)}, u32[]{:S(2)}, u32[]{:S(2)}) collective-permute-start(f32[19,34,18,1]{1,3,2,0:T(1,128)} %copy.158), channel_id=1, source_target_pairs={{1,0},{3,2},{5,4},{7,6},{9,8},{11,10},{13,12},{15,14},{17,16},{19,... | collective-permute-start | bytes 139544 | tf_op jit(solution)/shard_map/ppermute | solution.py:55
  431.9 6.5 %copy.159 = f32[19,34,18,1]{3,2,1,0:T(8,128)} copy(f32[19,34,18,1]{1,3,2,0:T(1,128)} %collective-permute-done.22) | data formatting | bytes 93024 | tf_op jit(solution)/shard_map/ppermute | solution.py:54
  438.4 6.2 %copy.160 = f32[19,34,18,1]{3,2,1,0:T(8,128)} copy(f32[19,34,18,1]{1,3,2,0:T(1,128)} %collective-permute-done.23) | data formatting | bytes 93024 | tf_op jit(solution)/shard_map/ppermute | solution.py:55
  444.6 13.0 %pad_maximum_fusion.3 = f32[19,34,18,66]{3,2,1,0:T(8,128)S(1)} fusion(f32[19,34,18,1]{3,2,1,0:T(8,128)} %copy.160, f32[19,34,1,64]{3,2,1,0:T(1,128)} %copy-done.54, f32[19,1,16,64]{3,2,1,0:T(8,128)} %copy-done.48, f32[19,32,16,64]{3,2,1,0:T(8,128)} %copy-done, f32[19,1,16,64]{3,2,1,0:T(8,128)S(1)} %collective-permute-done.18, ...), kind=kLoop, calls=%fused_computation.15 | loop fusion | flops 4604688 | bytes 6139584 | tf_op jit(solution)/shard_map/concatenate | solution.py:56
  (340 shorter events, 248.3 us)
Async XLA Ops:
  3.0 32.1 %collective-permute-start.2 = (s32[2,3]{1,0:T(2,128)S(1)}, s32[2,3]{1,0:T(2,128)S(1)}, u32[]{:S(2)}, u32[]{:S(2)}) collective-permute-start(s32[2,3]{1,0:T(2,128)S(1)} %slice.906), channel_id=1, source_target_pairs={{0,8},{8,16},{16,24},{24,32},{32,40},{40,48},{48,56},{56,64},{64,7... | collective-permute-start | bytes 80 | tf_op jit(solution)/shard_map/ppermute | solution.py:44
  5.7 35.1 %collective-permute-start = (s32[2,3]{1,0:T(2,128)S(1)}, s32[2,3]{1,0:T(2,128)S(1)}, u32[]{:S(2)}, u32[]{:S(2)}) collective-permute-start(s32[2,3]{1,0:T(2,128)S(1)} %slice.901), channel_id=1, source_target_pairs={{8,0},{16,8},{24,16},{32,24},{40,32},{48,40},{56,48},{64,56},{72,6... | collective-permute-start | bytes 80 | tf_op jit(solution)/shard_map/ppermute | solution.py:44
  10.4 30.6 %collective-permute-start.1 = (s32[2,4096]{1,0:T(2,128)S(1)}, s32[2,4096]{1,0:T(2,128)S(1)}, u32[]{:S(2)}, u32[]{:S(2)}) collective-permute-start(s32[2,4096]{1,0:T(2,128)S(1)} %slice.1121), channel_id=1, source_target_pairs={{8,0},{16,8},{24,16},{32,24},{40,32},{48,40},{56,48},{64,56},{72,6... | collective-permute-start | bytes 98312 | tf_op jit(solution)/shard_map/ppermute | solution.py:44
  13.7 28.1 %collective-permute-start.3 = (s32[2,4096]{1,0:T(2,128)S(1)}, s32[2,4096]{1,0:T(2,128)S(1)}, u32[]{:S(2)}, u32[]{:S(2)}) collective-permute-start(s32[2,4096]{1,0:T(2,128)S(1)} %slice.1122), channel_id=1, source_target_pairs={{0,8},{8,16},{16,24},{24,32},{32,40},{40,48},{48,56},{56,64},{64,7... | collective-permute-start | bytes 98312 | tf_op jit(solution)/shard_map/ppermute | solution.py:44
  25.0 55.8 %collective-permute-start.4 = (f32[2,19,4096]{2,0,1:T(2,128)S(1)}, f32[2,19,4096]{2,0,1:T(2,128)}, u32[]{:S(2)}, u32[]{:S(2)}) collective-permute-start(f32[2,19,4096]{2,0,1:T(2,128)S(1)} %copy.106), channel_id=1, source_target_pairs={{8,0},{16,8},{24,16},{32,24},{40,32},{48,40},{56,48},{64,56},{72,6... | collective-permute-start | bytes 1867784 | tf_op jit(solution)/shard_map/ppermute | solution.py:44
  35.1 49.8 %collective-permute-start.5 = (f32[2,19,4096]{2,0,1:T(2,128)}, f32[2,19,4096]{2,0,1:T(2,128)}, u32[]{:S(2)}, u32[]{:S(2)}) collective-permute-start(f32[2,19,4096]{2,0,1:T(2,128)} %copy.108), channel_id=1, source_target_pairs={{0,8},{8,16},{16,24},{24,32},{32,40},{40,48},{48,56},{56,64},{64,7... | collective-permute-start | bytes 1867784 | tf_op jit(solution)/shard_map/ppermute | solution.py:44
  44.1 13.0 %copy-start.46 = (s32[32,16,64]{2,1,0:T(8,128)}, s32[32,16,64]{2,1,0:T(8,128)S(1)}, u32[]{:S(2)}) copy-start(s32[32,16,64]{2,1,0:T(8,128)S(1)} %reshape.4210) | copy-start | bytes 393220
  44.1 8.1 %collective-permute-start.6 = (s32[1,16,64]{2,1,0:T(8,128)S(1)}, s32[1,16,64]{2,1,0:T(8,128)S(1)}, u32[]{:S(2)}, u32[]{:S(2)}) collective-permute-start(s32[1,16,64]{2,1,0:T(8,128)S(1)} %get-tuple-element.118), channel_id=1, source_target_pairs={{0,8},{8,16},{16,24},{24,32},{32,40},{40,48},{48,56},{56,64},{64,7... | collective-permute-start | bytes 12296 | tf_op jit(solution)/shard_map/ppermute | solution.py:54
  46.1 6.5 %collective-permute-start.7 = (s32[1,16,64]{2,1,0:T(8,128)S(1)}, s32[1,16,64]{2,1,0:T(8,128)S(1)}, u32[]{:S(2)}, u32[]{:S(2)}) collective-permute-start(s32[1,16,64]{2,1,0:T(8,128)S(1)} %get-tuple-element.117), channel_id=1, source_target_pairs={{8,0},{16,8},{24,16},{32,24},{40,32},{48,40},{56,48},{64,56},{72,6... | collective-permute-start | bytes 12296 | tf_op jit(solution)/shard_map/ppermute | solution.py:55
  52.6 4.5 collective-permute-start.8
  55.8 4.5 collective-permute-start.9
  60.6 19.9 %collective-permute-start.10 = (s32[34,18,1]{2,1,0:T(8,128)S(1)}, s32[34,18,1]{2,1,0:T(8,128)S(1)}, u32[]{:S(2)}, u32[]{:S(2)}) collective-permute-start(s32[34,18,1]{2,1,0:T(8,128)S(1)} %get-tuple-element.113), channel_id=1, source_target_pairs={{0,1},{2,3},{4,5},{6,7},{8,9},{10,11},{12,13},{14,15},{16,17},{18,... | collective-permute-start | bytes 7352 | tf_op jit(solution)/shard_map/ppermute | solution.py:54
  61.9 18.6 %collective-permute-start.11 = (s32[34,18,1]{2,1,0:T(8,128)S(1)}, s32[34,18,1]{2,1,0:T(8,128)S(1)}, u32[]{:S(2)}, u32[]{:S(2)}) collective-permute-start(s32[34,18,1]{2,1,0:T(8,128)S(1)} %get-tuple-element.114), channel_id=1, source_target_pairs={{1,0},{3,2},{5,4},{7,6},{9,8},{11,10},{13,12},{15,14},{17,16},{19,... | collective-permute-start | bytes 7352 | tf_op jit(solution)/shard_map/ppermute | solution.py:55
  232.8 32.8 %copy-start.1 = (f32[19,32,16,64]{3,2,1,0:T(8,128)}, f32[19,32,16,64]{3,2,1,0:T(8,128)S(1)}, u32[]{:S(2)}) copy-start(f32[19,32,16,64]{3,2,1,0:T(8,128)S(1)} %fusion.151) | copy-start | bytes 7471108
  232.8 9.1 %collective-permute-start.12 = (f32[19,1,16,64]{3,2,1,0:T(8,128)S(1)}, f32[19,1,16,64]{3,2,1,0:T(8,128)S(1)}, u32[]{:S(2)}, u32[]{:S(2)}) collective-permute-start(f32[19,1,16,64]{3,2,1,0:T(8,128)S(1)} %get-tuple-element.108), channel_id=1, source_target_pairs={{0,8},{8,16},{16,24},{24,32},{32,40},{40,48},{48,56},{56,64},{64,7... | collective-permute-start | bytes 233480 | tf_op jit(solution)/shard_map/ppermute | solution.py:54
  238.3 10.0 %collective-permute-start.13 = (f32[19,1,16,64]{3,2,1,0:T(8,128)S(1)}, f32[19,1,16,64]{3,2,1,0:T(8,128)S(1)}, u32[]{:S(2)}, u32[]{:S(2)}) collective-permute-start(f32[19,1,16,64]{3,2,1,0:T(8,128)S(1)} %get-tuple-element.109), channel_id=1, source_target_pairs={{8,0},{16,8},{24,16},{32,24},{40,32},{48,40},{56,48},{64,56},{72,6... | collective-permute-start | bytes 233480 | tf_op jit(solution)/shard_map/ppermute | solution.py:55
  248.8 9.7 %collective-permute-start.14 = (f32[19,34,1,64]{3,2,1,0:T(1,128)S(1)}, f32[19,34,1,64]{3,2,1,0:T(1,128)S(1)}, u32[]{:S(2)}, u32[]{:S(2)}) collective-permute-start(f32[19,34,1,64]{3,2,1,0:T(1,128)S(1)} %get-tuple-element.104), channel_id=1, source_target_pairs={{0,2},{2,4},{4,6},{1,3},{3,5},{5,7},{8,10},{10,12},{12,14},{9,11},... | collective-permute-start | bytes 496136 | tf_op jit(solution)/shard_map/ppermute | solution.py:54
  252.0 10.4 %collective-permute-start.15 = (f32[19,34,1,64]{3,2,1,0:T(1,128)S(1)}, f32[19,34,1,64]{3,2,1,0:T(1,128)S(1)}, u32[]{:S(2)}, u32[]{:S(2)}) collective-permute-start(f32[19,34,1,64]{3,2,1,0:T(1,128)S(1)} %get-tuple-element.105), channel_id=1, source_target_pairs={{2,0},{4,2},{6,4},{3,1},{5,3},{7,5},{10,8},{12,10},{14,12},{11,9},... | collective-permute-start | bytes 496136 | tf_op jit(solution)/shard_map/ppermute | solution.py:55
  283.9 59.5 %collective-permute-start.17 = (f32[19,34,18,1]{1,3,2,0:T(1,128)S(1)}, f32[19,34,18,1]{1,3,2,0:T(1,128)}, u32[]{:S(2)}, u32[]{:S(2)}) collective-permute-start(f32[19,34,18,1]{1,3,2,0:T(1,128)S(1)} %copy.133), channel_id=1, source_target_pairs={{1,0},{3,2},{5,4},{7,6},{9,8},{11,10},{13,12},{15,14},{17,16},{19,... | collective-permute-start | bytes 139544 | tf_op jit(solution)/shard_map/ppermute | solution.py:55
  288.1 49.0 %collective-permute-start.16 = (f32[19,34,18,1]{1,3,2,0:T(1,128)}, f32[19,34,18,1]{1,3,2,0:T(1,128)}, u32[]{:S(2)}, u32[]{:S(2)}) collective-permute-start(f32[19,34,18,1]{1,3,2,0:T(1,128)} %copy.132), channel_id=1, source_target_pairs={{0,1},{2,3},{4,5},{6,7},{8,9},{10,11},{12,13},{14,15},{16,17},{18,... | collective-permute-start | bytes 139544 | tf_op jit(solution)/shard_map/ppermute | solution.py:54
  303.6 8.5 %copy-start.4 = (f32[1,2,16,1,16,4,16]{6,5,4,2,1,3,0:T(4,128)S(1)}, f32[1,2,16,1,16,4,16]{6,5,4,2,1,3,0:T(4,128)}, u32[]{:S(2)}) copy-start(f32[1,2,16,1,16,4,16]{6,5,4,2,1,3,0:T(4,128)} %copy.121) | copy-start | bytes 393220
  304.8 8.5 %copy-start.5 = (f32[1,2,16,1,16,4,16]{6,5,4,2,1,3,0:T(4,128)S(1)}, f32[1,2,16,1,16,4,16]{6,5,4,2,1,3,0:T(4,128)}, u32[]{:S(2)}) copy-start(f32[1,2,16,1,16,4,16]{6,5,4,2,1,3,0:T(4,128)} %copy.120) | copy-start | bytes 393220
  313.3 8.4 %copy-start.6 = (f32[1,2,16,1,16,4,16]{6,5,4,2,1,3,0:T(4,128)S(1)}, f32[1,2,16,1,16,4,16]{6,5,4,2,1,3,0:T(4,128)}, u32[]{:S(2)}) copy-start(f32[1,2,16,1,16,4,16]{6,5,4,2,1,3,0:T(4,128)} %copy.116) | copy-start | bytes 393220
  324.1 11.0 %copy-start.45 = (f32[2,16,16,4,16]{4,2,1,3,0:T(8,128)S(1)}, f32[2,16,16,4,16]{4,2,1,3,0:T(8,128)}, u32[]{:S(2)}) copy-start(f32[2,16,16,4,16]{4,2,1,3,0:T(8,128)} %get-tuple-element.112) | copy-start | bytes 393220
  379.4 24.8 %copy-start = (f32[19,32,16,64]{3,2,1,0:T(8,128)}, f32[19,32,16,64]{3,2,1,0:T(8,128)S(1)}, u32[]{:S(2)}) copy-start(f32[19,32,16,64]{3,2,1,0:T(8,128)S(1)} %fusion.323) | copy-start | bytes 7471108
  379.4 6.0 %collective-permute-start.18 = (f32[19,1,16,64]{3,2,1,0:T(8,128)S(1)}, f32[19,1,16,64]{3,2,1,0:T(8,128)S(1)}, u32[]{:S(2)}, u32[]{:S(2)}) collective-permute-start(f32[19,1,16,64]{3,2,1,0:T(8,128)S(1)} %get-tuple-element.106), channel_id=1, source_target_pairs={{0,8},{8,16},{16,24},{24,32},{32,40},{40,48},{48,56},{56,64},{64,7... | collective-permute-start | bytes 233480 | tf_op jit(solution)/shard_map/ppermute | solution.py:54
  381.3 8.1 %collective-permute-start.19 = (f32[19,1,16,64]{3,2,1,0:T(8,128)S(1)}, f32[19,1,16,64]{3,2,1,0:T(8,128)S(1)}, u32[]{:S(2)}, u32[]{:S(2)}) collective-permute-start(f32[19,1,16,64]{3,2,1,0:T(8,128)S(1)} %get-tuple-element.107), channel_id=1, source_target_pairs={{8,0},{16,8},{24,16},{32,24},{40,32},{48,40},{56,48},{64,56},{72,6... | collective-permute-start | bytes 233480 | tf_op jit(solution)/shard_map/ppermute | solution.py:55
  389.4 14.8 %copy-start.48 = (f32[19,1,16,64]{3,2,1,0:T(8,128)}, f32[19,1,16,64]{3,2,1,0:T(8,128)S(1)}, u32[]{:S(2)}) copy-start(f32[19,1,16,64]{3,2,1,0:T(8,128)S(1)} %collective-permute-done.19) | copy-start | bytes 233476
  390.0 7.2 %collective-permute-start.20 = (f32[19,34,1,64]{3,2,1,0:T(1,128)S(1)}, f32[19,34,1,64]{3,2,1,0:T(1,128)S(1)}, u32[]{:S(2)}, u32[]{:S(2)}) collective-permute-start(f32[19,34,1,64]{3,2,1,0:T(1,128)S(1)} %get-tuple-element.102), channel_id=1, source_target_pairs={{0,2},{2,4},{4,6},{1,3},{3,5},{5,7},{8,10},{10,12},{12,14},{9,11},... | collective-permute-start | bytes 496136 | tf_op jit(solution)/shard_map/ppermute | solution.py:54
  393.1 7.9 %collective-permute-start.21 = (f32[19,34,1,64]{3,2,1,0:T(1,128)S(1)}, f32[19,34,1,64]{3,2,1,0:T(1,128)S(1)}, u32[]{:S(2)}, u32[]{:S(2)}) collective-permute-start(f32[19,34,1,64]{3,2,1,0:T(1,128)S(1)} %get-tuple-element.103), channel_id=1, source_target_pairs={{2,0},{4,2},{6,4},{3,1},{5,3},{7,5},{10,8},{12,10},{14,12},{11,9},... | collective-permute-start | bytes 496136 | tf_op jit(solution)/shard_map/ppermute | solution.py:55
  417.1 14.9 %collective-permute-start.22 = (f32[19,34,18,1]{1,3,2,0:T(1,128)}, f32[19,34,18,1]{1,3,2,0:T(1,128)}, u32[]{:S(2)}, u32[]{:S(2)}) collective-permute-start(f32[19,34,18,1]{1,3,2,0:T(1,128)} %copy.157), channel_id=1, source_target_pairs={{0,1},{2,3},{4,5},{6,7},{8,9},{10,11},{12,13},{14,15},{16,17},{18,... | collective-permute-start | bytes 139544 | tf_op jit(solution)/shard_map/ppermute | solution.py:54
  424.3 14.1 %collective-permute-start.23 = (f32[19,34,18,1]{1,3,2,0:T(1,128)}, f32[19,34,18,1]{1,3,2,0:T(1,128)}, u32[]{:S(2)}, u32[]{:S(2)}) collective-permute-start(f32[19,34,18,1]{1,3,2,0:T(1,128)} %copy.158), channel_id=1, source_target_pairs={{1,0},{3,2},{5,4},{7,6},{9,8},{11,10},{13,12},{15,14},{17,16},{19,... | collective-permute-start | bytes 139544 | tf_op jit(solution)/shard_map/ppermute | solution.py:55
  (51 other events, 143.9 us)
where the time goes:
time: 479 us; the launch traced here: 469 us
  local copies, waits for them, and re-layouts  280 us (58%)
  other arithmetic  78.5 us (16%)
  starting transfers between devices  74.3 us (16%)
  waiting for transfers between devices  34.4 us (7%)
    slice x10, local copies, waits for them, and re-layouts, moment(): summed = summed - lattice[member]  38 us
    squeeze x18, local copies, waits for them, and re-layouts, moment(): summed = summed + lattice[member]  36.6 us
    squeeze x18, local copies, waits for them, and re-layouts, moment(): summed = summed - lattice[member]  36.5 us
    concatenate x5, other arithmetic, with_halo(): shard = jnp.concatenate([before, shard, after], axis=dim)  32 us
    ppermute x9, starting transfers between devices, with_halo(): after = lax.ppermute(first, axis, down)  31.2 us
    unnamed x54, other arithmetic  28.2 us
    slice x8, local copies, waits for them, and re-layouts, with_halo(): last = lax.slice_in_dim(shard, length - width, length, axis=dim)  25.8 us
    slice x9, local copies, waits for them, and re-layouts, moment(): summed = summed + lattice[member]  25 us
  transfers between devices with their start and end apart: 24, of which 11 were waited for; matrix products, arithmetic and copies ran while one was open for 22% of the time, Pallas kernels for 0%

commit v1 on v0

v1 whole, which is shorter than its diff:
```python
import jax
import jax.numpy as jnp
from jax import lax
from jax.experimental import pallas as pl
from jax.experimental.pallas import tpu as pltpu
from jax.sharding import PartitionSpec as P

MESH = pl.DeviceIdType.MESH
F32 = jnp.float32

GROUPS = (
    (0, 0, 0, 5, 6),
    (1, 0, 1, 11, 13),
    (-1, 0, 2, 14, 12),
    (0, 1, 3, 15, 17),
    (0, -1, 4, 18, 16),
)
DIAGONALS = ((1, 1, 7), (-1, -1, 8), (1, -1, 9), (-1, 1, 10))
PAIRS = ((1, 2), (3, 4), (5, 6), (7, 8), (9, 10), (11, 12), (13, 14), (15, 16), (17, 18))
OPPOSITE = (0, 2, 1, 4, 3, 6, 5, 8, 7, 10, 9, 12, 11, 14, 13, 16, 15, 18, 17)
UP_X = (1, 7, 9, 11, 13)
DOWN_X = (2, 8, 10, 12, 14)
UP_Y = (3, 7, 10, 15, 17)
DOWN_Y = (4, 8, 9, 16, 18)
MARK = 19

EDGE = 16
CHUNKS = 4
PLANES = EDGE // CHUNKS
TILES = 2 * PLANES
ROWS = 12
OMEGA = 0.2 / 192.0


def roll(value, shift, axis=1):
    return pltpu.roll(value, shift % value.shape[axis] if isinstance(shift, int) else shift, axis)


def collide(f, mark):
    plus = [f[i] + f[o] for i, o in PAIRS]
    minus = [f[i] - f[o] for i, o in PAIRS]
    density = f[0] + ((plus[0] + plus[1]) + (plus[2] + plus[3])) + (
        (plus[4] + plus[5]) + (plus[6] + plus[7]) + plus[8]
    )
    mx = (minus[0] + minus[3]) + (minus[4] + minus[5]) + minus[6]
    my = (minus[1] + minus[3]) - (minus[4] - minus[7]) + minus[8]
    mz = (minus[2] + minus[5]) - (minus[6] - minus[7]) - minus[8]
    inverse = 1.0 / density
    base = density - 1.5 * (mx * mx + my * my + mz * mz) * inverse
    squared = 4.5 * inverse
    along = (mx, my, mz, mx + my, mx - my, mx + mz, mx - mz, my + mz, my - mz)
    post = [None] * 19
    post[0] = f[0] - 1.25 * (f[0] - (1.0 / 3.0) * base)
    for k, (i, o) in enumerate(PAIRS):
        weight = 1.0 / 18.0 if k < 3 else 1.0 / 36.0
        m = along[k]
        even = 0.625 * plus[k] - (1.25 * weight) * (base + squared * (m * m))
        odd = (4.0 / 9.0) * minus[k] - (8.0 / 3.0 * weight) * m
        post[i] = f[i] - even - odd
        post[o] = f[o] - even + odd
    return [jnp.where(mark, f[i], post[i]) for i in range(19)], density


def group_swap(values):
    lane = lax.broadcasted_iota(jnp.int32, values[0].shape, 1)
    for bit in range(3):
        step = 1 << bit
        high = (lane // (16 * step)) % 2 == 1
        out = list(values)
        for i in range(8):
            if i & step:
                continue
            low_one, high_one = values[i], values[i + step]
            out[i] = jnp.where(high, roll(high_one, 16 * step), low_one)
            out[i + step] = jnp.where(high, high_one, roll(low_one, -16 * step))
        values = out
    return values


def kernel(pos, held, mark_in, out, held_marks, send, recv, stage, ext1, ext2, rho, walls,
           rotors, face_x, face_y, face_z, edge_xy, edge_yz, edge_xz,
           got_x, got_y, got_z, got_xy, got_yz, got_xz, zext,
           move_send, move_recv, halo_send, halo_recv):
    s = lax.axis_index("stream")
    cy = lax.axis_index("cy")
    core = lax.axis_index("cz")
    n_s = lax.axis_size("stream")
    n_y = lax.axis_size("cy")
    up_s, down_s = lax.rem(s + 1, n_s), lax.rem(s + n_s - 1, n_s)
    up_y, down_y = lax.rem(cy + 1, n_y), lax.rem(cy + n_y - 1, n_y)
    other = 1 - core
    partners = (
        (up_s, cy, core), (down_s, cy, core), (s, up_y, core), (s, down_y, core), (s, cy, other),
        (up_s, up_y, core), (down_s, down_y, core), (up_s, down_y, core), (down_s, up_y, core),
        (s, up_y, other), (s, down_y, other), (up_s, cy, other), (down_s, cy, other),
    )

    barrier = pltpu.get_barrier_semaphore()
    for partner in partners:
        pl.semaphore_signal(barrier, inc=1, device_id=partner, device_id_type=MESH)

    source = [jnp.int32(-1)] * 8
    up_row = [jnp.int32(0), jnp.int32(0)]
    down_row = [jnp.int32(0), jnp.int32(0)]
    up_low, up_high = jnp.int32(99), jnp.int32(-1)
    down_low, down_high = jnp.int32(99), jnp.int32(-1)
    for r in range(ROWS):
        bx = pos[0, r]
        layer = bx - 2 * s
        bz = pos[2, r] - 4 * core
        spot = jnp.where((layer >= 0) & (layer < 2) & (bx >= 0), layer * 4 + bz, -1)
        source = [jnp.where(spot == j, r, source[j]) for j in range(8)]
        rises = layer >= 2
        sinks = (layer < 0) & (bx >= 0)
        less, more = rises & (bz < up_low), rises & (bz > up_high)
        up_row = [jnp.where(less, r, up_row[0]), jnp.where(more, r, up_row[1])]
        up_low, up_high = jnp.where(less, bz, up_low), jnp.where(more, bz, up_high)
        less, more = sinks & (bz < down_low), sinks & (bz > down_high)
        down_row = [jnp.where(less, r, down_row[0]), jnp.where(more, r, down_row[1])]
        down_low, down_high = jnp.where(less, bz, down_low), jnp.where(more, bz, down_high)
    order = []
    for layer in range(2):
        missing = jnp.int32(0)
        for z in range(4):
            order.append(jnp.minimum(missing, 1))
            missing = missing + jnp.where(source[layer * 4 + z] < 0, 1, 0)
    here = [jnp.full((8, 128), source[j], jnp.int32) >= 0 for j in range(8)]
    here4 = [jnp.full((4, 128), source[j], jnp.int32) >= 0 for j in range(8)]
    later = [jnp.full((8, 128), order[j], jnp.int32) > 0 for j in range(8)]
    second = [jnp.full((4, 128), order[j], jnp.int32) > 0 for j in range(8)]
    source = [jnp.maximum(source[j], 0) for j in range(8)]

    for r in range(ROWS):
        held_marks[r] = mark_in[r:r + 1, :].astype(F32)

    def cells(k):
        return pl.ds(pl.multiple_of(k * 128, 128), 128)

    def tail(row, k):
        marks = held_marks[row, :, cells(k)]
        return jnp.concatenate([held[row, 16:19, cells(k)], marks], axis=0)

    def move(d, c):
        return pltpu.make_async_remote_copy(
            src_ref=send.at[d, c], dst_ref=recv.at[d, c],
            send_sem=move_send.at[d, c], recv_sem=move_recv.at[d, c],
            device_id=partners[d], device_id_type=MESH,
        )

    def pack(c):
        @pl.loop(0, TILES)
        def _(kk):
            k = c * TILES + kk
            for d, rows in ((0, up_row), (1, down_row)):
                for q in range(2):
                    send[d, c, kk, 2 * q] = held[rows[q], 0:8, cells(k)]
                    send[d, c, kk, 2 * q + 1] = held[rows[q], 8:16, cells(k)]
                send[d, c, kk, 4] = jnp.concatenate(
                    [tail(rows[0], k), tail(rows[1], k)], axis=0)

    for c in range(CHUNKS):
        pack(c)
        if c == 0:
            pl.semaphore_wait(barrier, len(partners))
        move(0, c).start()
        move(1, c).start()

    lane = lax.broadcasted_iota(jnp.int32, (8, 128), 1)
    low_half = lane < 64

    def settle(c, carry):
        move(0, c).wait_recv()
        move(1, c).wait_recv()

        @pl.loop(0, PLANES)
        def _(plane):
            a = c * PLANES + plane
            for h in range(2):
                kk = plane * 2 + h
                k = c * TILES + kk
                for t in range(3):
                    tiles = []
                    for j in range(8):
                        d = j // 4
                        if t < 2:
                            mine = held[source[j], 8 * t:8 * t + 8, cells(k)]
                            theirs = jnp.where(later[j], recv[d, c, kk, 2 + t], recv[d, c, kk, t])
                            tiles.append(jnp.where(here[j], mine, theirs))
                        else:
                            theirs = recv[d, c, kk, 4]
                            theirs = jnp.where(second[j], theirs[4:8], theirs[0:4])
                            tiles.append(jnp.where(here4[j], tail(source[j], k), theirs))
                    height = tiles[0].shape[0]
                    for g, value in enumerate(group_swap(tiles)):
                        stage[t, 8 * g:8 * g + height, :] = value
                f = [stage[p // 8, pl.ds(p % 8, 8, stride=8), :] for p in range(19)]
                marks = stage[2, pl.ds(3, 8, stride=8), :]
                post, density = collide(f, marks > 0.5)
                for p in range(19):
                    ext1[p, a + 1, 8 + 8 * h:16 + 8 * h, :] = post[p]
                ext1[MARK, a + 1, 8 + 8 * h:16 + 8 * h, :] = marks
                rho[a, 8 * h:8 * h + 8, :] = density
        return carry

    lax.fori_loop(0, CHUNKS, settle, 0)

    z_edge = jnp.where(core == 0, 63, 0)
    sent_z = [jnp.where(core == 0, group[3], group[4]) for group in GROUPS] + [MARK]
    flat_lane = lane % 64

    def messages(step):
        n = 6 if step == 0 else 5
        refs = []
        for d in range(2):
            refs.append((face_x.at[step, d, pl.ds(0, n)], got_x.at[step, d, pl.ds(0, n)]))
        for d in range(2):
            refs.append((face_y.at[step, d, pl.ds(0, n)], got_y.at[step, d, pl.ds(0, n)]))
        refs.append((face_z.at[step, pl.ds(0, n)], got_z.at[step, pl.ds(0, n)]))
        for e in range(4):
            refs.append((edge_xy.at[step, e], got_xy.at[step, e]))
        for e in range(2):
            refs.append((edge_yz.at[step, e], got_yz.at[step, e]))
        for e in range(2):
            refs.append((edge_xz.at[step, e], got_xz.at[step, e]))
        return [
            pltpu.make_async_remote_copy(
                src_ref=src, dst_ref=dst, send_sem=halo_send.at[step, i],
                recv_sem=halo_recv.at[step, i], device_id=partners[i], device_id_type=MESH,
            )
            for i, (src, dst) in enumerate(refs)
        ]

    def exchange(ext, step):
        n = 6 if step == 0 else 5
        flat = ext.reshape(20, 18 * 32, 128)
        for d, pops in ((0, UP_X), (1, DOWN_X)):
            plane = 16 if d == 0 else 1
            for j, p in enumerate((pops + (MARK,))[:n]):
                for h in range(2):
                    face_x[step, d, j, 8 * h:8 * h + 8, :] = roll(
                        ext[p, plane, 8 + 8 * h:16 + 8 * h, :], 64)
        for d, pops in ((0, UP_Y), (1, DOWN_Y)):
            row = 23 if d == 0 else 8
            for j, p in enumerate((pops + (MARK,))[:n]):
                for h in range(2):
                    face_y[step, d, j, 8 * h:8 * h + 8, :] = flat[
                        p, pl.ds(32 * (1 + 8 * h) + row, 8, stride=32), :]

        def gather(a, totals):
            shift = lax.rem(a + 1 - z_edge + 128, 128)
            keep = flat_lane == a + 1
            return tuple(
                jnp.where(keep, roll(ext[sent_z[j], a + 1, 8 + 8 * h:16 + 8 * h, :], shift),
                          totals[2 * j + h])
                for j in range(n) for h in range(2)
            )

        zero = jnp.zeros((8, 128), F32)
        totals = lax.fori_loop(0, EDGE, gather, (zero,) * (2 * n))
        for j in range(n):
            for h in range(2):
                face_z[step, j, 8 * h:8 * h + 8, :] = totals[2 * j + h]
        for e, (d, j, row) in enumerate(((0, 1, 15), (1, 1, 0), (0, 2, 0), (1, 2, 15))):
            edge_xy[step, e, 0:1, :] = face_x[step, d, j, row:row + 1, :]
            if step == 0:
                edge_xy[step, e, 1:2, :] = face_x[step, d, 5, row:row + 1, :]
        for e, (j, row) in enumerate(((3, 15), (4, 0))):
            edge_yz[step, e, 0:1, :] = face_z[step, j, row:row + 1, :]
            if step == 0:
                edge_yz[step, e, 1:2, :] = face_z[step, 5, row:row + 1, :]
        for e, j in enumerate((1, 2)):
            for h in range(2):
                value = totals[2 * j + h]
                if step == 0:
                    at = 80 if e == 0 else 1
                    value = jnp.where(lane == at, value, roll(totals[10 + h], 1))
                edge_xz[step, e, 8 * h:8 * h + 8, :] = value

        copies = messages(step)
        for copy in copies:
            copy.start()
        for copy in copies:
            copy.wait_recv()

        for d, pops, row in ((0, UP_Y, 7), (1, DOWN_Y, 24)):
            outside = (cy == 0) if d == 0 else (cy == n_y - 1)
            for j, p in enumerate((pops + (MARK,))[:n]):
                for h in range(2):
                    value = got_y[step, d, j, 8 * h:8 * h + 8, :]
                    if p == MARK:
                        value = jnp.where(outside, jnp.full_like(value, 2.0), value)
                    flat[p, pl.ds(32 * (1 + 8 * h) + row, 8, stride=32), :] = value
        for d, pops in ((0, UP_X), (1, DOWN_X)):
            plane, behind = (0, 16) if d == 0 else (17, 1)
            beyond = low_half if d == 0 else jnp.logical_not(low_half)
            outside = (s == 0) if d == 0 else (s == n_s - 1)
            for j, p in enumerate((pops + (MARK,))[:n]):
                for h in range(2):
                    value = got_x[step, d, j, 8 * h:8 * h + 8, :]
                    if p == MARK:
                        value = jnp.where(outside, jnp.full_like(value, 2.0), value)
                    ext[p, plane, 8 + 8 * h:16 + 8 * h, :] = jnp.where(
                        beyond, value, face_x[step, d, j, 8 * h:8 * h + 8, :])
        for e, (d, p, row) in enumerate(((0, 7, 7), (1, 8, 24), (0, 9, 24), (1, 10, 7))):
            plane, behind = (0, 16) if d == 0 else (17, 1)
            beyond = (low_half if d == 0 else jnp.logical_not(low_half))[0:1]
            own = roll(ext[p, behind, row:row + 1, :], 64)
            ext[p, plane, row:row + 1, :] = jnp.where(beyond, got_xy[step, e, 0:1, :], own)
            if step == 0:
                out_x = (s == 0) if d == 0 else (s == n_s - 1)
                out_y = (cy == 0) if row == 7 else (cy == n_y - 1)
                value = got_xy[step, e, 1:2, :]
                value = jnp.where(out_x | out_y, jnp.full_like(value, 2.0), value)
                own = roll(ext[MARK, behind, row:row + 1, :], 64)
                ext[MARK, plane, row:row + 1, :] = jnp.where(beyond, value, own)
        for j in range(n):
            low_side = j in (1, 5)
            high_side = j in (2, 5)
            for h in range(2):
                value = got_z[step, j, 8 * h:8 * h + 8, :]
                fixed = value
                if low_side:
                    far = roll(got_xz[step, 0, 8 * h:8 * h + 8, :], 128 - (80 if j == 1 else 81))
                    if j == 5:
                        far = jnp.where(s == 0, jnp.full_like(far, 2.0), far)
                    fixed = jnp.where(lane == 64, roll(value, 48), fixed)
                    fixed = jnp.where(lane == 0, far, fixed)
                if high_side:
                    far = roll(got_xz[step, 1, 8 * h:8 * h + 8, :], 80 if j == 2 else 79)
                    if j == 5:
                        far = jnp.where(s == n_s - 1, jnp.full_like(far, 2.0), far)
                    fixed = jnp.where(lane == 17, roll(value, 80), fixed)
                    fixed = jnp.where(lane == 81, far, fixed)
                zext[step, j, 8 + 8 * h:16 + 8 * h, :] = fixed
        zext[step, 3, 7:8, :] = got_yz[step, 0, 0:1, :]
        zext[step, 4, 24:25, :] = got_yz[step, 1, 0:1, :]
        if step == 0:
            for e, row in ((0, 7), (1, 24)):
                outside = (cy == 0) if e == 0 else (cy == n_y - 1)
                value = got_yz[step, e, 1:2, :]
                zext[step, 5, row:row + 1, :] = jnp.where(
                    outside, jnp.full_like(value, 2.0), value)
        for copy in copies:
            copy.wait_send()

    first_z = flat_lane == 0
    last_z = flat_lane == 63
    z_target = jnp.where(core == 1, 0, 63)

    def rows(h, step_y):
        start = 8 + 8 * h - step_y
        return slice(start, start + 8)

    def z_halo(step, j, a, h, step_x, step_y):
        shift = lax.rem(z_target - a + (127 + step_x), 128)
        return roll(zext[step, j, rows(h, step_y), :], shift)

    def make_bits(a, carry):
        for h in range(2):
            wall = jnp.zeros((8, 128), jnp.int32)
            rotor = jnp.zeros((8, 128), jnp.int32)

            def add(bit, value):
                nonlocal wall, rotor
                wall = wall + jnp.where(value > 0.5, 1 << bit, 0)
                if bit > 2:
                    rotor = rotor + jnp.where(value == 1.0, 1 << bit, 0)

            for step_x, step_y, p_flat, p_up, p_down in GROUPS:
                value = ext1[MARK, a + 1 - step_x, rows(h, step_y), :]
                add(p_flat, value)
                halo = z_halo(0, 5, a, h, step_x, step_y)
                add(p_up, jnp.where(
                    first_z, jnp.where(core == 1, halo, jnp.full_like(halo, 2.0)), roll(value, 1)))
                add(p_down, jnp.where(
                    last_z, jnp.where(core == 0, halo, jnp.full_like(halo, 2.0)), roll(value, -1)))
            for step_x, step_y, p in DIAGONALS:
                add(p, ext1[MARK, a + 1 - step_x, rows(h, step_y), :])
            walls[a, 8 * h:8 * h + 8, :] = wall
            rotors[a, 8 * h:8 * h + 8, :] = rotor
        return carry

    along_z = (core * 64 + flat_lane).astype(F32) - 63.5
    drift_a = (-OMEGA / 6.0) * along_z
    sub = lax.broadcasted_iota(jnp.int32, (8, 128), 0)

    def pull(ext, step, a, h):
        here_rows = slice(8 + 8 * h, 16 + 8 * h)
        centre = [ext[p, a + 1, here_rows, :] for p in range(19)]
        wall = walls[a, 8 * h:8 * h + 8, :]
        rotor = rotors[a, 8 * h:8 * h + 8, :]
        density = rho[a, 8 * h:8 * h + 8, :]
        along_y = (cy * 16 + 8 * h + sub).astype(F32) - 31.5
        push_a = density * drift_a
        push_b = density * ((OMEGA / 6.0) * along_y)
        both, apart = push_a + push_b, push_a - push_b
        push = {
            3: 2.0 * push_a, 4: -2.0 * push_a, 5: 2.0 * push_b, 6: -2.0 * push_b,
            7: push_a, 8: -push_a, 9: -push_a, 10: push_a,
            11: push_b, 12: -push_b, 13: -push_b, 14: push_b,
            15: both, 16: -both, 17: apart, 18: -apart,
        }
        solid = (wall & 1) != 0
        new = [None] * 19
        new[0] = centre[0]

        def settle_one(p, pulled):
            bounced = centre[OPPOSITE[p]]
            if p > 2:
                bounced = bounced + jnp.where((rotor & (1 << p)) != 0, push[p], 0.0)
            value = jnp.where((wall & (1 << p)) != 0, bounced, pulled)
            new[p] = jnp.where(solid, centre[p], value)

        for j, (step_x, step_y, p_flat, p_up, p_down) in enumerate(GROUPS):
            if p_flat:
                settle_one(p_flat, ext[p_flat, a + 1 - step_x, rows(h, step_y), :])
            halo = z_halo(step, j, a, h, step_x, step_y)
            value = ext[p_up, a + 1 - step_x, rows(h, step_y), :]
            settle_one(p_up, jnp.where(first_z, halo, roll(value, 1)))
            value = ext[p_down, a + 1 - step_x, rows(h, step_y), :]
            settle_one(p_down, jnp.where(last_z, halo, roll(value, -1)))
        for step_x, step_y, p in DIAGONALS:
            settle_one(p, ext[p, a + 1 - step_x, rows(h, step_y), :])
        return new, solid

    exchange(ext1, 0)
    lax.fori_loop(0, EDGE, make_bits, 0)

    def middle(a, carry):
        for h in range(2):
            new, solid = pull(ext1, 0, a, h)
            post, density = collide(new, solid)
            for p in range(19):
                ext2[p, a + 1, 8 + 8 * h:16 + 8 * h, :] = post[p]
            rho[a, 8 * h:8 * h + 8, :] = density
        return carry

    lax.fori_loop(0, EDGE, middle, 0)
    exchange(ext2, 1)

    def last(a, carry):
        for h in range(2):
            new, _ = pull(ext2, 1, a, h)
            for p in range(19):
                out[p, a, 8 * h:8 * h + 8, :] = new[p][:, 0:64]
                out[p, EDGE + a, 8 * h:8 * h + 8, :] = roll(new[p], 64)[:, 0:64]
        return carry

    lax.fori_loop(0, EDGE, last, 0)
    for c in range(CHUNKS):
        move(0, c).wait_send()
        move(1, c).wait_send()


def step_all(populations, solid_cells, block_pos):
    scratch = [
        pltpu.VMEM((ROWS, 1, 4096), F32),
        pltpu.VMEM((2, CHUNKS, TILES, 5, 8, 128), F32),
        pltpu.VMEM((2, CHUNKS, TILES, 5, 8, 128), F32),
        pltpu.VMEM((3, 64, 128), F32),
        pltpu.VMEM((20, 18, 32, 128), F32),
        pltpu.VMEM((20, 18, 32, 128), F32),
        pltpu.VMEM((EDGE, 16, 128), F32),
        pltpu.VMEM((EDGE, 16, 128), jnp.int32),
        pltpu.VMEM((EDGE, 16, 128), jnp.int32),
    ]
    for _ in range(2):
        scratch += [
            pltpu.VMEM((2, 2, 6, 16, 128), F32),
            pltpu.VMEM((2, 2, 6, 16, 128), F32),
            pltpu.VMEM((2, 6, 16, 128), F32),
            pltpu.VMEM((2, 4, 8, 128), F32),
            pltpu.VMEM((2, 2, 8, 128), F32),
            pltpu.VMEM((2, 2, 16, 128), F32),
        ]
    scratch += [
        pltpu.VMEM((2, 6, 32, 128), F32),
        pltpu.SemaphoreType.DMA((2, CHUNKS)),
        pltpu.SemaphoreType.DMA((2, CHUNKS)),
        pltpu.SemaphoreType.DMA((2, 13)),
        pltpu.SemaphoreType.DMA((2, 13)),
    ]
    return pl.pallas_call(
        kernel,
        out_shape=jax.ShapeDtypeStruct((19, 32, 16, 64), F32),
        in_specs=[
            pl.BlockSpec(memory_space=pltpu.SMEM),
            pl.BlockSpec(memory_space=pltpu.VMEM),
            pl.BlockSpec(memory_space=pltpu.VMEM),
        ],
        out_specs=pl.BlockSpec(memory_space=pltpu.VMEM),
        scratch_shapes=scratch,
        compiler_params=pltpu.CompilerParams(
            collective_id=0, has_side_effects=True, vmem_limit_bytes=40 * 1024 * 1024
        ),
    )(block_pos.T, populations, solid_cells)


def solution(mesh):
    in_specs = (
        P(("stream", "cy", "cz"), None, None),
        P(("stream", "cy", "cz"), None),
        P(("stream", "cy", "cz"), None),
    )
    out_specs = P(None, "stream", "cy", "cz")
    return jax.shard_map(step_all, mesh=mesh, in_specs=in_specs, out_specs=out_specs, check_vma=False)
```

time: 479 us -> 55.7 us (0.12)
  the two profiles are of different devices: /device:TPU:99 before, /device:TPU:1 now
where the time goes in v1:
time: 55.7 us; the launch traced here: 55.5 us
  Pallas kernels  49.3 us (89%)
  local copies, waits for them, and re-layouts  6.24 us (11%)
    pallas_call x1, Pallas kernels, step_all(): pl.pallas_call(kernel, out_shape=jax.ShapeDtypeStruct((19, 32, 16, 64), F...  49.3 us
    unnamed x7, local copies, waits for them, and re-layouts  6.24 us

profile of v1, /device:TPU:1, one launch (start us, length us, event | category | flops | bytes accessed | tf_op | source)
XLA Modules:
  0.0 55.5 jit_solution(7384102194057072792)
XLA Ops:
  0.0 0.0 copy-start
  0.0 2.3 %copy-done = f32[12,19,4096]{2,1,0:T(8,128)S(1)} copy-done((f32[12,19,4096]{2,1,0:T(8,128)S(1)}, f32[12,19,4096]{2,1,0:T(8,128)}, u32[]{:S(2)}) %copy-start) | copy-done | bytes 3735576
  2.3 0.0 copy-start.1
  2.3 0.9 %copy-done.1 = s32[12,4096]{1,0:T(8,128)S(1)} copy-done((s32[12,4096]{1,0:T(8,128)S(1)}, s32[12,4096]{1,0:T(8,128)}, u32[]{:S(2)}) %copy-start.1) | copy-done | bytes 196632
  3.3 0.0 copy-start.2
  3.3 0.7 %copy-done.2 = s32[12,3]{0,1:T(4,128)S(1)} copy-done((s32[12,3]{0,1:T(4,128)S(1)}, s32[12,3]{0,1:T(4,128)}, u32[]{:S(2)}) %copy-start.2) | copy-done | bytes 168
  4.0 49.3 %shard_map.37 = f32[19,32,16,64]{3,2,1,0:T(8,128)S(1)} custom-call(s32[3,12]{1,0:T(4,128)S(1)} %bitcast.1, f32[12,19,4096]{2,1,0:T(8,128)S(1)} %copy-done, s32[12,4096]{1,0:T(8,128)S(1)} %copy-done.1), custom_call_target="tpu_custom_call" | custom-call | tf_op jit(solution)/shard_map/pallas_call | solution.py:483
  53.2 2.3 %copy.5 = f32[19,32,16,64]{3,2,1,0:T(8,128)} copy(f32[19,32,16,64]{3,2,1,0:T(8,128)S(1)} %shard_map.37) | data formatting | bytes 4980736
Async XLA Ops:
  0.0 2.3 %copy-start = (f32[12,19,4096]{2,1,0:T(8,128)S(1)}, f32[12,19,4096]{2,1,0:T(8,128)}, u32[]{:S(2)}) copy-start(f32[12,19,4096]{2,1,0:T(8,128)} %held.1) | copy-start | bytes 11206660
  2.3 0.9 %copy-start.1 = (s32[12,4096]{1,0:T(8,128)S(1)}, s32[12,4096]{1,0:T(8,128)}, u32[]{:S(2)}) copy-start(s32[12,4096]{1,0:T(8,128)} %mark_in.1) | copy-start | bytes 589828
  3.3 0.7 %copy-start.2 = (s32[12,3]{0,1:T(4,128)S(1)}, s32[12,3]{0,1:T(4,128)}, u32[]{:S(2)}) copy-start(s32[12,3]{0,1:T(4,128)} %param.5) | copy-start | bytes 436

commit v2 on v1

v2 whole, which is shorter than its diff:
```python
import jax
import jax.numpy as jnp
from jax import lax
from jax.experimental import pallas as pl
from jax.experimental.pallas import tpu as pltpu
from jax.sharding import PartitionSpec as P

MESH = pl.DeviceIdType.MESH
F32 = jnp.float32

GROUPS = (
    (0, 0, 0, 5, 6),
    (1, 0, 1, 11, 13),
    (-1, 0, 2, 14, 12),
    (0, 1, 3, 15, 17),
    (0, -1, 4, 18, 16),
)
DIAGONALS = ((1, 1, 7), (-1, -1, 8), (1, -1, 9), (-1, 1, 10))
PAIRS = ((1, 2), (3, 4), (5, 6), (7, 8), (9, 10), (11, 12), (13, 14), (15, 16), (17, 18))
OPPOSITE = (0, 2, 1, 4, 3, 6, 5, 8, 7, 10, 9, 12, 11, 14, 13, 16, 15, 18, 17)
UP_X = (1, 7, 9, 11, 13)
DOWN_X = (2, 8, 10, 12, 14)
UP_Y = (3, 7, 10, 15, 17)
DOWN_Y = (4, 8, 9, 16, 18)
MARK = 19

EDGE = 16
CHUNKS = 8
TILES = 4
OUTER = 7
ROWS = 12
OMEGA = 0.2 / 192.0
REVERSE = (1, 0, 3, 2, 4, 6, 5, 8, 7, 10, 9, 12, 11)


def roll(value, shift, axis=1):
    return pltpu.roll(value, shift % value.shape[axis] if isinstance(shift, int) else shift, axis)


def collide(f, mark):
    plus = [f[i] + f[o] for i, o in PAIRS]
    minus = [f[i] - f[o] for i, o in PAIRS]
    density = f[0] + ((plus[0] + plus[1]) + (plus[2] + plus[3])) + (
        (plus[4] + plus[5]) + (plus[6] + plus[7]) + plus[8]
    )
    mx = (minus[0] + minus[3]) + (minus[4] + minus[5]) + minus[6]
    my = (minus[1] + minus[3]) - (minus[4] - minus[7]) + minus[8]
    mz = (minus[2] + minus[5]) - (minus[6] - minus[7]) - minus[8]
    inverse = 1.0 / density
    base = density - 1.5 * (mx * mx + my * my + mz * mz) * inverse
    squared = 4.5 * inverse
    along = (mx, my, mz, mx + my, mx - my, mx + mz, mx - mz, my + mz, my - mz)
    post = [None] * 19
    post[0] = f[0] - 1.25 * (f[0] - (1.0 / 3.0) * base)
    for k, (i, o) in enumerate(PAIRS):
        weight = 1.0 / 18.0 if k < 3 else 1.0 / 36.0
        m = along[k]
        even = 0.625 * plus[k] - (1.25 * weight) * (base + squared * (m * m))
        odd = (4.0 / 9.0) * minus[k] - (8.0 / 3.0 * weight) * m
        post[i] = f[i] - even - odd
        post[o] = f[o] - even + odd
    return [jnp.where(mark, f[i], post[i]) for i in range(19)], density


def group_swap(values):
    lane = lax.broadcasted_iota(jnp.int32, values[0].shape, 1)
    for bit in range(3):
        step = 1 << bit
        high = (lane // (16 * step)) % 2 == 1
        out = list(values)
        for i in range(8):
            if i & step:
                continue
            low_one, high_one = values[i], values[i + step]
            out[i] = jnp.where(high, roll(high_one, 16 * step), low_one)
            out[i + step] = jnp.where(high, high_one, roll(low_one, -16 * step))
        values = out
    return values


def kernel(pos_in, pop_in, mark_in, out, held, marks_in, held_marks, pos, send, recv, stage, ext1, ext2,
           rho, walls, rotors, face_x, face_y, late_y, face_z, edge_xy, edge_yz, edge_xz,
           got_x, got_y, got_late_y, got_z, got_xy, got_yz, got_xz, zext,
           in_sem, move_send, move_recv, halo_send, halo_recv):
    s = lax.axis_index("stream")
    cy = lax.axis_index("cy")
    core = lax.axis_index("cz")
    n_s = lax.axis_size("stream")
    n_y = lax.axis_size("cy")
    up_s, down_s = lax.rem(s + 1, n_s), lax.rem(s + n_s - 1, n_s)
    up_y, down_y = lax.rem(cy + 1, n_y), lax.rem(cy + n_y - 1, n_y)
    other = 1 - core
    partners = (
        (up_s, cy, core), (down_s, cy, core), (s, up_y, core), (s, down_y, core), (s, cy, other),
        (up_s, up_y, core), (down_s, down_y, core), (up_s, down_y, core), (down_s, up_y, core),
        (s, up_y, other), (s, down_y, other), (up_s, cy, other), (down_s, cy, other),
    )
    above_s, below_s = s < n_s - 1, s > 0
    above_y, below_y = cy < n_y - 1, cy > 0
    exists = (
        above_s, below_s, above_y, below_y, None,
        above_s & above_y, below_s & below_y, above_s & below_y, below_s & above_y,
        above_y, below_y, above_s, below_s,
    )

    def when(condition, act):
        if condition is None:
            act()
        else:
            pl.when(condition)(act)

    loads = [pltpu.make_async_copy(pos_in, pos, in_sem.at[0]),
             pltpu.make_async_copy(mark_in, marks_in, in_sem.at[1])]
    loads += [
        pltpu.make_async_copy(pop_in.at[pl.ds(3 * i, 3)], held.at[pl.ds(3 * i, 3)], in_sem.at[2 + i])
        for i in range(4)
    ]
    for load in loads:
        load.start()
    barrier = pltpu.get_barrier_semaphore()
    arrivals = jnp.int32(0)
    for i, partner in enumerate(partners):
        when(exists[i], lambda partner=partner: pl.semaphore_signal(
            barrier, inc=1, device_id=partner, device_id_type=MESH))
        arrivals = arrivals + (1 if exists[i] is None else jnp.where(exists[i], 1, 0))

    loads[0].wait()
    source = [jnp.int32(-1)] * 8
    up_row = [jnp.int32(0), jnp.int32(0)]
    down_row = [jnp.int32(0), jnp.int32(0)]
    up_low, up_high = jnp.int32(99), jnp.int32(-1)
    down_low, down_high = jnp.int32(99), jnp.int32(-1)
    for r in range(ROWS):
        bx = pos[0, r]
        layer = bx - 2 * s
        bz = pos[2, r] - 4 * core
        spot = jnp.where((layer >= 0) & (layer < 2) & (bx >= 0), layer * 4 + bz, -1)
        source = [jnp.where(spot == j, r, source[j]) for j in range(8)]
        rises = layer >= 2
        sinks = (layer < 0) & (bx >= 0)
        less, more = rises & (bz < up_low), rises & (bz > up_high)
        up_row = [jnp.where(less, r, up_row[0]), jnp.where(more, r, up_row[1])]
        up_low, up_high = jnp.where(less, bz, up_low), jnp.where(more, bz, up_high)
        less, more = sinks & (bz < down_low), sinks & (bz > down_high)
        down_row = [jnp.where(less, r, down_row[0]), jnp.where(more, r, down_row[1])]
        down_low, down_high = jnp.where(less, bz, down_low), jnp.where(more, bz, down_high)
    order = []
    for layer in range(2):
        missing = jnp.int32(0)
        for z in range(4):
            order.append(jnp.minimum(missing, 1))
            missing = missing + jnp.where(source[layer * 4 + z] < 0, 1, 0)
    here = [jnp.full((8, 128), source[j], jnp.int32) >= 0 for j in range(8)]
    here4 = [jnp.full((4, 128), source[j], jnp.int32) >= 0 for j in range(8)]
    later = [jnp.full((8, 128), order[j], jnp.int32) > 0 for j in range(8)]
    second = [jnp.full((4, 128), order[j], jnp.int32) > 0 for j in range(8)]
    source = [jnp.maximum(source[j], 0) for j in range(8)]

    for load in loads[1:]:
        load.wait()
    for r in range(ROWS):
        held_marks[r] = marks_in[r:r + 1, :].astype(F32)

    def plane_of(pair, side):
        return pair + side * (15 - 2 * pair)

    def cells(k):
        return pl.ds(pl.multiple_of(k * 128, 128), 128)

    def tail(row, k):
        return jnp.concatenate([held[row, 16:19, cells(k)], held_marks[row, :, cells(k)]], axis=0)

    def move(d, c):
        return pltpu.make_async_remote_copy(
            src_ref=send.at[d, c], dst_ref=recv.at[d, c],
            send_sem=move_send.at[d, c], recv_sem=move_recv.at[d, c],
            device_id=partners[d], device_id_type=MESH,
        )

    def pack(c):
        @pl.loop(0, TILES)
        def _(kk):
            k = 2 * plane_of(c, kk // 2) + kk % 2
            for d, rows in ((0, up_row), (1, down_row)):
                for q in range(2):
                    send[d, c, kk, 2 * q] = held[rows[q], 0:8, cells(k)]
                    send[d, c, kk, 2 * q + 1] = held[rows[q], 8:16, cells(k)]
                send[d, c, kk, 4] = jnp.concatenate(
                    [tail(rows[0], k), tail(rows[1], k)], axis=0)

    pack(0)
    pl.semaphore_wait(barrier, arrivals)
    for c in range(CHUNKS):
        if c:
            pack(c)
        for d in range(2):
            when(exists[d], lambda d=d, c=c: move(d, c).start())

    lane = lax.broadcasted_iota(jnp.int32, (8, 128), 1)
    low_half = lane < 64
    flat_lane = lane % 64
    z_edge = jnp.where(core == 0, 63, 0)
    sent_z = [jnp.where(core == 0, group[3], group[4]) for group in GROUPS] + [MARK]

    def count(step):
        return 6 if step == 0 else 5

    def late_planes(step):
        first = OUTER - step
        return first, 16 - 2 * first

    def late_rows(step):
        return -(-count(step) * late_planes(step)[1] // 8) * 8

    def message(step, kind, e):
        n = count(step)
        if kind == "x":
            i, src, dst, slot = e, face_x.at[step, e, pl.ds(0, n)], got_x.at[step, e, pl.ds(0, n)], e
        elif kind == "xy":
            i, src, dst, slot = 5 + e, edge_xy.at[step, e], got_xy.at[step, e], 2 + e
        elif kind == "xz":
            i, src, dst, slot = 11 + e, edge_xz.at[step, e], got_xz.at[step, e], 6 + e
        elif kind == "y0":
            i, src, dst = 2 + e, face_y.at[step, e, pl.ds(0, n)], got_y.at[step, e, pl.ds(0, n)]
            slot = 8 + e
        elif kind == "y1":
            rows = pl.ds(0, late_rows(step))
            i, src, dst = 2 + e, late_y.at[step, e, rows], got_late_y.at[step, e, rows]
            slot = 13 + e
        else:
            g = int(kind[-1])
            if kind[:-1] == "z":
                i, slot = 4, 10 + 5 * g
                src, dst = face_z.at[step, g, pl.ds(0, n)], got_z.at[step, g, pl.ds(0, n)]
            else:
                i, slot = 9 + e, 11 + 5 * g + e
                src, dst = edge_yz.at[step, g, e], got_yz.at[step, g, e]
        copy = pltpu.make_async_remote_copy(
            src_ref=src, dst_ref=dst, send_sem=halo_send.at[step, slot],
            recv_sem=halo_recv.at[step, slot], device_id=partners[i], device_id_type=MESH,
        )
        return copy, exists[i], exists[REVERSE[i]]

    def of_kind(step, *kinds):
        sizes = {"x": 2, "xy": 4, "xz": 2, "y0": 2, "y1": 2, "z0": 1, "z1": 1, "yz0": 2, "yz1": 2}
        return [message(step, kind, e) for kind in kinds for e in range(sizes[kind])]

    def start(step, *kinds):
        for copy, there, _ in of_kind(step, *kinds):
            when(there, copy.start)

    def arrive(step, *kinds):
        for copy, _, there in of_kind(step, *kinds):
            when(there, copy.wait_recv)

    def send_x(ext, step):
        n = count(step)
        for d, pops in ((0, UP_X), (1, DOWN_X)):
            plane = 16 if d == 0 else 1
            for j, p in enumerate((pops + (MARK,))[:n]):
                for h in range(2):
                    face_x[step, d, j, 8 * h:8 * h + 8, :] = roll(
                        ext[p, plane, 8 + 8 * h:16 + 8 * h, :], 64)
        for e, (d, j, row) in enumerate(((0, 1, 15), (1, 1, 0), (0, 2, 0), (1, 2, 15))):
            edge_xy[step, e, 0:1, :] = face_x[step, d, j, row:row + 1, :]
            if step == 0:
                edge_xy[step, e, 1:2, :] = face_x[step, d, 5, row:row + 1, :]
        for e, (j, plane) in enumerate(((1, 16), (2, 1))):
            shift = (64 - z_edge) if e == 0 else (128 + 81 - z_edge) % 128
            for h in range(2):
                rows = slice(8 + 8 * h, 16 + 8 * h)
                value = roll(ext[sent_z[j], plane, rows, :], shift)
                if step == 0:
                    marks = roll(roll(ext[MARK, plane, rows, :], shift), 1)
                    value = jnp.where(lane == (0 if e == 0 else 81), value, marks)
                edge_xz[step, e, 8 * h:8 * h + 8, :] = value
        start(step, "x", "xy", "xz")

    def send_yz(ext, step, late):
        n = count(step)
        flat = ext.reshape(20, 18 * 32, 128)
        first, planes = late_planes(step)
        for d, pops in ((0, UP_Y), (1, DOWN_Y)):
            row = 23 if d == 0 else 8
            for j, p in enumerate((pops + (MARK,))[:n]):
                if late:
                    late_y[step, d, j * planes:(j + 1) * planes, :] = flat[
                        p, pl.ds(32 * (1 + first) + row, planes, stride=32), :]
                else:
                    for h in range(2):
                        face_y[step, d, j, 8 * h:8 * h + 8, :] = flat[
                            p, pl.ds(32 * (1 + 8 * h) + row, 8, stride=32), :]
        start(step, "y1" if late else "y0")

        def gather(i, totals):
            a = first + i if late else i + (i // first) * planes
            shift = lax.rem(a + 1 - z_edge + 128, 128)
            keep = flat_lane == a + 1
            return tuple(
                jnp.where(keep, roll(ext[sent_z[j], a + 1, 8 + 8 * h:16 + 8 * h, :], shift),
                          totals[2 * j + h])
                for j in range(n) for h in range(2)
            )

        zero = jnp.zeros((8, 128), F32)
        totals = lax.fori_loop(0, planes if late else 2 * first, gather, (zero,) * (2 * n))
        for j in range(n):
            for h in range(2):
                face_z[step, late, j, 8 * h:8 * h + 8, :] = totals[2 * j + h]
        for e, (j, row) in enumerate(((3, 15), (4, 0))):
            edge_yz[step, late, e, 0:1, :] = face_z[step, late, j, row:row + 1, :]
            if step == 0:
                edge_yz[step, late, e, 1:2, :] = face_z[step, late, 5, row:row + 1, :]
        start(step, "yz1" if late else "yz0", "z1" if late else "z0")

    def outside_or(condition, value):
        return jnp.where(condition, jnp.full_like(value, 2.0), value)

    def take_yz(ext, step, late):
        n = count(step)
        flat = ext.reshape(20, 18 * 32, 128)
        first, planes = late_planes(step)
        if late:
            arrive(step, "z1", "y1", "yz1")
        else:
            arrive(step, "z0", "y0", "yz0")
        for d, pops, row in ((0, UP_Y, 7), (1, DOWN_Y, 24)):
            outside = (cy == 0) if d == 0 else (cy == n_y - 1)
            for j, p in enumerate((pops + (MARK,))[:n]):
                if late:
                    value = got_late_y[step, d, j * planes:(j + 1) * planes, :]
                    if p == MARK:
                        value = outside_or(outside, value)
                    flat[p, pl.ds(32 * (1 + first) + row, planes, stride=32), :] = value
                else:
                    for h in range(2):
                        value = got_y[step, d, j, 8 * h:8 * h + 8, :]
                        if p == MARK:
                            value = outside_or(outside, value)
                        flat[p, pl.ds(32 * (1 + 8 * h) + row, 8, stride=32), :] = value
        fresh = (flat_lane > first) & (flat_lane <= first + planes)

        def merge(j, rows, value):
            if late:
                value = jnp.where(fresh[0:value.shape[0]], value, zext[step, j, rows, :])
            zext[step, j, rows, :] = value

        for j in range(n):
            for h in range(2):
                value = got_z[step, late, j, 8 * h:8 * h + 8, :]
                if not late:
                    fixed = value
                    if j in (1, 5):
                        fixed = jnp.where(lane == 64, roll(value, 48), fixed)
                    if j in (2, 5):
                        fixed = jnp.where(lane == 17, roll(value, 80), fixed)
                    value = fixed
                merge(j, slice(8 + 8 * h, 16 + 8 * h), value)
        merge(3, slice(7, 8), got_yz[step, late, 0, 0:1, :])
        merge(4, slice(24, 25), got_yz[step, late, 1, 0:1, :])
        if step == 0:
            for e, row in ((0, 7), (1, 24)):
                outside = (cy == 0) if e == 0 else (cy == n_y - 1)
                merge(5, slice(row, row + 1), outside_or(outside, got_yz[step, late, e, 1:2, :]))

    def take_x(ext, step):
        n = count(step)
        arrive(step, "x", "xy", "xz")
        for d, pops in ((0, UP_X), (1, DOWN_X)):
            plane = 0 if d == 0 else 17
            beyond = low_half if d == 0 else jnp.logical_not(low_half)
            outside = (s == 0) if d == 0 else (s == n_s - 1)
            for j, p in enumerate((pops + (MARK,))[:n]):
                for h in range(2):
                    value = got_x[step, d, j, 8 * h:8 * h + 8, :]
                    if p == MARK:
                        value = outside_or(outside, value)
                    ext[p, plane, 8 + 8 * h:16 + 8 * h, :] = jnp.where(
                        beyond, value, face_x[step, d, j, 8 * h:8 * h + 8, :])
        for e, (d, p, row) in enumerate(((0, 7, 7), (1, 8, 24), (0, 9, 24), (1, 10, 7))):
            plane, behind = (0, 16) if d == 0 else (17, 1)
            beyond = (low_half if d == 0 else jnp.logical_not(low_half))[0:1]
            own = roll(ext[p, behind, row:row + 1, :], 64)
            ext[p, plane, row:row + 1, :] = jnp.where(beyond, got_xy[step, e, 0:1, :], own)
            if step == 0:
                out_x = (s == 0) if d == 0 else (s == n_s - 1)
                out_y = (cy == 0) if row == 7 else (cy == n_y - 1)
                value = outside_or(out_x | out_y, got_xy[step, e, 1:2, :])
                own = roll(ext[MARK, behind, row:row + 1, :], 64)
                ext[MARK, plane, row:row + 1, :] = jnp.where(beyond, value, own)
        for e, (j, at) in enumerate(((1, 0), (2, 81))):
            outside = (s == 0) if e == 0 else (s == n_s - 1)
            for h in range(2):
                rows = slice(8 + 8 * h, 16 + 8 * h)
                value = got_xz[step, e, 8 * h:8 * h + 8, :]
                zext[step, j, rows, :] = jnp.where(lane == at, value, zext[step, j, rows, :])
                if step == 0:
                    marks = outside_or(outside, roll(value, -1))
                    zext[step, 5, rows, :] = jnp.where(lane == at, marks, zext[step, 5, rows, :])

    def settle(c, carry):
        for d in range(2):
            when(exists[1 - d], lambda d=d: move(d, c).wait_recv())

        @pl.loop(0, 2)
        def _(side):
            a = plane_of(c, side)
            for h in range(2):
                kk = side * 2 + h
                k = 2 * a + h
                for t in range(3):
                    tiles = []
                    for j in range(8):
                        d = j // 4
                        if t < 2:
                            mine = held[source[j], 8 * t:8 * t + 8, cells(k)]
                            theirs = jnp.where(later[j], recv[d, c, kk, 2 + t], recv[d, c, kk, t])
                            tiles.append(jnp.where(here[j], mine, theirs))
                        else:
                            theirs = recv[d, c, kk, 4]
                            theirs = jnp.where(second[j], theirs[4:8], theirs[0:4])
                            tiles.append(jnp.where(here4[j], tail(source[j], k), theirs))
                    height = tiles[0].shape[0]
                    for g, value in enumerate(group_swap(tiles)):
                        stage[t, 8 * g:8 * g + height, :] = value
                f = [stage[p // 8, pl.ds(p % 8, 8, stride=8), :] for p in range(19)]
                marks = stage[2, pl.ds(3, 8, stride=8), :]
                post, density = collide(f, marks > 0.5)
                for p in range(19):
                    ext1[p, a + 1, 8 + 8 * h:16 + 8 * h, :] = post[p]
                ext1[MARK, a + 1, 8 + 8 * h:16 + 8 * h, :] = marks
                rho[a, 8 * h:8 * h + 8, :] = density

        pl.when(c == 0)(lambda: send_x(ext1, 0))
        pl.when(c == OUTER - 1)(lambda: send_yz(ext1, 0, 0))
        return carry

    lax.fori_loop(0, CHUNKS, settle, 0)
    send_yz(ext1, 0, 1)

    first_z = flat_lane == 0
    last_z = flat_lane == 63
    z_target = jnp.where(core == 1, 0, 63)

    def rows(h, step_y):
        start_row = 8 + 8 * h - step_y
        return slice(start_row, start_row + 8)

    def z_halo(step, j, a, h, step_x, step_y):
        shift = lax.rem(z_target - a + (127 + step_x), 128)
        return roll(zext[step, j, rows(h, step_y), :], shift)

    def make_bits(a, h):
        wall = jnp.zeros((8, 128), jnp.int32)
        rotor = jnp.zeros((8, 128), jnp.int32)

        def add(bit, value):
            nonlocal wall, rotor
            wall = wall + jnp.where(value > 0.5, 1 << bit, 0)
            if bit > 2:
                rotor = rotor + jnp.where(value == 1.0, 1 << bit, 0)

        for step_x, step_y, p_flat, p_up, p_down in GROUPS:
            value = ext1[MARK, a + 1 - step_x, rows(h, step_y), :]
            add(p_flat, value)
            halo = z_halo(0, 5, a, h, step_x, step_y)
            add(p_up, jnp.where(first_z, outside_or(core == 0, halo), roll(value, 1)))
            add(p_down, jnp.where(last_z, outside_or(core == 1, halo), roll(value, -1)))
        for step_x, step_y, p in DIAGONALS:
            add(p, ext1[MARK, a + 1 - step_x, rows(h, step_y), :])
        walls[a, 8 * h:8 * h + 8, :] = wall
        rotors[a, 8 * h:8 * h + 8, :] = rotor
        return wall, rotor

    along_z = (core * 64 + flat_lane).astype(F32) - 63.5
    drift_a = (-OMEGA / 6.0) * along_z
    sub = lax.broadcasted_iota(jnp.int32, (8, 128), 0)

    def pull(ext, step, a, h, wall, rotor):
        here_rows = slice(8 + 8 * h, 16 + 8 * h)
        centre = [ext[p, a + 1, here_rows, :] for p in range(19)]
        density = rho[a, 8 * h:8 * h + 8, :]
        along_y = (cy * 16 + 8 * h + sub).astype(F32) - 31.5
        push_a = density * drift_a
        push_b = density * ((OMEGA / 6.0) * along_y)
        both, apart = push_a + push_b, push_a - push_b
        push = {
            3: 2.0 * push_a, 4: -2.0 * push_a, 5: 2.0 * push_b, 6: -2.0 * push_b,
            7: push_a, 8: -push_a, 9: -push_a, 10: push_a,
            11: push_b, 12: -push_b, 13: -push_b, 14: push_b,
            15: both, 16: -both, 17: apart, 18: -apart,
        }
        solid = (wall & 1) != 0
        new = [None] * 19
        new[0] = centre[0]

        def settle_one(p, pulled):
            bounced = centre[OPPOSITE[p]]
            if p > 2:
                bounced = bounced + jnp.where((rotor & (1 << p)) != 0, push[p], 0.0)
            value = jnp.where((wall & (1 << p)) != 0, bounced, pulled)
            new[p] = jnp.where(solid, centre[p], value)

        for j, (step_x, step_y, p_flat, p_up, p_down) in enumerate(GROUPS):
            if p_flat:
                settle_one(p_flat, ext[p_flat, a + 1 - step_x, rows(h, step_y), :])
            halo = z_halo(step, j, a, h, step_x, step_y)
            value = ext[p_up, a + 1 - step_x, rows(h, step_y), :]
            settle_one(p_up, jnp.where(first_z, halo, roll(value, 1)))
            value = ext[p_down, a + 1 - step_x, rows(h, step_y), :]
            settle_one(p_down, jnp.where(last_z, halo, roll(value, -1)))
        for step_x, step_y, p in DIAGONALS:
            settle_one(p, ext[p, a + 1 - step_x, rows(h, step_y), :])
        return new, solid

    take_yz(ext1, 0, 0)
    take_x(ext1, 0)

    def middle(i, carry):
        @pl.when(i == 2)
        def _():
            send_x(ext2, 1)

        @pl.when(i == 2 * (OUTER - 1))
        def _():
            send_yz(ext2, 1, 0)
            take_yz(ext1, 0, 1)

        a = plane_of(i // 2, i % 2)
        for h in range(2):
            wall, rotor = make_bits(a, h)
            new, solid = pull(ext1, 0, a, h, wall, rotor)
            post, density = collide(new, solid)
            for p in range(19):
                ext2[p, a + 1, 8 + 8 * h:16 + 8 * h, :] = post[p]
            rho[a, 8 * h:8 * h + 8, :] = density
        return carry

    lax.fori_loop(0, EDGE, middle, 0)
    send_yz(ext2, 1, 1)
    take_yz(ext2, 1, 0)

    def last(i, carry):
        @pl.when(i == 2 * (OUTER - 3))
        def _():
            take_yz(ext2, 1, 1)

        @pl.when(i == 14)
        def _():
            take_x(ext2, 1)

        a = plane_of((i // 2 + 1) % 8, i % 2)
        for h in range(2):
            wall = walls[a, 8 * h:8 * h + 8, :]
            rotor = rotors[a, 8 * h:8 * h + 8, :]
            new, _ = pull(ext2, 1, a, h, wall, rotor)
            for p in range(19):
                out[p, a, 8 * h:8 * h + 8, :] = new[p][:, 0:64]
                out[p, EDGE + a, 8 * h:8 * h + 8, :] = roll(new[p], 64)[:, 0:64]
        return carry

    lax.fori_loop(0, EDGE, last, 0)
    for c in range(CHUNKS):
        for d in range(2):
            when(exists[d], lambda d=d, c=c: move(d, c).wait_send())
    for step in range(2):
        for copy, there, _ in of_kind(step, "x", "xy", "xz", "y0", "y1", "z0", "z1", "yz0", "yz1"):
            when(there, copy.wait_send)


def step_all(populations, solid_cells, block_pos):
    scratch = [
        pltpu.VMEM((ROWS, 19, 4096), F32),
        pltpu.VMEM((ROWS, 4096), jnp.int32),
        pltpu.VMEM((ROWS, 1, 4096), F32),
        pltpu.SMEM((3, ROWS), jnp.int32),
        pltpu.VMEM((2, CHUNKS, TILES, 5, 8, 128), F32),
        pltpu.VMEM((2, CHUNKS, TILES, 5, 8, 128), F32),
        pltpu.VMEM((3, 64, 128), F32),
        pltpu.VMEM((20, 18, 32, 128), F32),
        pltpu.VMEM((20, 18, 32, 128), F32),
        pltpu.VMEM((EDGE, 16, 128), F32),
        pltpu.VMEM((EDGE, 16, 128), jnp.int32),
        pltpu.VMEM((EDGE, 16, 128), jnp.int32),
    ]
    for _ in range(2):
        scratch += [
            pltpu.VMEM((2, 2, 6, 16, 128), F32),
            pltpu.VMEM((2, 2, 6, 16, 128), F32),
            pltpu.VMEM((2, 2, 48, 128), F32),
            pltpu.VMEM((2, 2, 6, 16, 128), F32),
            pltpu.VMEM((2, 4, 8, 128), F32),
            pltpu.VMEM((2, 2, 2, 8, 128), F32),
            pltpu.VMEM((2, 2, 16, 128), F32),
        ]
    scratch += [
        pltpu.VMEM((2, 6, 32, 128), F32),
        pltpu.SemaphoreType.DMA((6,)),
        pltpu.SemaphoreType.DMA((2, CHUNKS)),
        pltpu.SemaphoreType.DMA((2, CHUNKS)),
        pltpu.SemaphoreType.DMA((2, 18)),
        pltpu.SemaphoreType.DMA((2, 18)),
    ]
    return pl.pallas_call(
        kernel,
        out_shape=jax.ShapeDtypeStruct((19, 32, 16, 64), F32),
        in_specs=[pl.BlockSpec(memory_space=pltpu.HBM)] * 3,
        out_specs=pl.BlockSpec(memory_space=pltpu.VMEM),
        scratch_shapes=scratch,
        compiler_params=pltpu.CompilerParams(
            collective_id=0, has_side_effects=True, vmem_limit_bytes=40 * 1024 * 1024
        ),
    )(*(pltpu.with_memory_space_constraint(value, pltpu.HBM)
        for value in (block_pos.T, populations, solid_cells)))


def solution(mesh):
    in_specs = (
        P(("stream", "cy", "cz"), None, None),
        P(("stream", "cy", "cz"), None),
        P(("stream", "cy", "cz"), None),
    )
    out_specs = P(None, "stream", "cy", "cz")
    return jax.shard_map(step_all, mesh=mesh, in_specs=in_specs, out_specs=out_specs, check_vma=False)
```

time: 55.7 us -> 39.1 us (0.70)
  the two profiles are of different devices: /device:TPU:1 before, /device:TPU:7 now
where the time goes in v2:
time: 39.1 us; the launch traced here: 39 us
  Pallas kernels  36.7 us (94%)
  local copies, waits for them, and re-layouts  2.27 us (6%)
    pallas_call x1, Pallas kernels, step_all(): pl.pallas_call(kernel, out_shape=jax.ShapeDtypeStruct((19, 32, 16, 64), F...  36.7 us
    unnamed x1, local copies, waits for them, and re-layouts  2.27 us

profile of v2, /device:TPU:7, one launch (start us, length us, event | category | flops | bytes accessed | tf_op | source)
XLA Modules:
  0.0 39.0 jit_solution(18352179761603883269)
XLA Ops:
  0.0 36.7 %shard_map.37 = f32[19,32,16,64]{3,2,1,0:T(8,128)S(1)} custom-call(s32[3,12]{1,0:T(4,128)} %bitcast.1, f32[12,19,4096]{2,1,0:T(8,128)} %pop_in.1, s32[12,4096]{1,0:T(8,128)} %mark_in.1), custom_call_target="tpu_custom_call" | custom-call | tf_op jit(solution)/shard_map/pallas_call | solution.py:604
  36.7 2.3 %copy.5 = f32[19,32,16,64]{3,2,1,0:T(8,128)} copy(f32[19,32,16,64]{3,2,1,0:T(8,128)S(1)} %shard_map.37) | data formatting | bytes 4980736

commit v3 on v2

--- a/solution.py
+++ b/solution.py
@@ -27,7 +27,6 @@
 EDGE = 16
 CHUNKS = 8
 TILES = 4
-OUTER = 7
 ROWS = 12
 OMEGA = 0.2 / 192.0
 REVERSE = (1, 0, 3, 2, 4, 6, 5, 8, 7, 10, 9, 12, 11)
@@ -79,9 +78,9 @@
 
 
 def kernel(pos_in, pop_in, mark_in, out, held, marks_in, held_marks, pos, send, recv, stage, ext1, ext2,
-           rho, walls, rotors, face_x, face_y, late_y, face_z, edge_xy, edge_yz, edge_xz,
-           got_x, got_y, got_late_y, got_z, got_xy, got_yz, got_xz, zext,
-           in_sem, move_send, move_recv, halo_send, halo_recv):
+           rho, walls, rotors, face_x, face_y, face_z, edge_xy, edge_yz, edge_xz,
+           got_x, got_y, got_z, got_xy, got_yz, got_xz, zext,
+           in_sem, move_send, move_recv, x_send, x_recv, pair_send, pair_recv):
     s = lax.axis_index("stream")
     cy = lax.axis_index("cy")
     core = lax.axis_index("cz")
@@ -201,57 +200,84 @@
     flat_lane = lane % 64
     z_edge = jnp.where(core == 0, 63, 0)
     sent_z = [jnp.where(core == 0, group[3], group[4]) for group in GROUPS] + [MARK]
+    edge_shift = [lax.rem(128 + j - z_edge, 128) for j in range(6)]
 
     def count(step):
         return 6 if step == 0 else 5
 
-    def late_planes(step):
-        first = OUTER - step
-        return first, 16 - 2 * first
-
-    def late_rows(step):
-        return -(-count(step) * late_planes(step)[1] // 8) * 8
-
-    def message(step, kind, e):
-        n = count(step)
-        if kind == "x":
-            i, src, dst, slot = e, face_x.at[step, e, pl.ds(0, n)], got_x.at[step, e, pl.ds(0, n)], e
-        elif kind == "xy":
-            i, src, dst, slot = 5 + e, edge_xy.at[step, e], got_xy.at[step, e], 2 + e
-        elif kind == "xz":
-            i, src, dst, slot = 11 + e, edge_xz.at[step, e], got_xz.at[step, e], 6 + e
-        elif kind == "y0":
-            i, src, dst = 2 + e, face_y.at[step, e, pl.ds(0, n)], got_y.at[step, e, pl.ds(0, n)]
-            slot = 8 + e
-        elif kind == "y1":
-            rows = pl.ds(0, late_rows(step))
-            i, src, dst = 2 + e, late_y.at[step, e, rows], got_late_y.at[step, e, rows]
-            slot = 13 + e
-        else:
-            g = int(kind[-1])
-            if kind[:-1] == "z":
-                i, slot = 4, 10 + 5 * g
-                src, dst = face_z.at[step, g, pl.ds(0, n)], got_z.at[step, g, pl.ds(0, n)]
-            else:
-                i, slot = 9 + e, 11 + 5 * g + e
-                src, dst = edge_yz.at[step, g, e], got_yz.at[step, g, e]
+    def remote(src, dst, sems, i):
         copy = pltpu.make_async_remote_copy(
-            src_ref=src, dst_ref=dst, send_sem=halo_send.at[step, slot],
-            recv_sem=halo_recv.at[step, slot], device_id=partners[i], device_id_type=MESH,
+            src_ref=src, dst_ref=dst, send_sem=sems[0], recv_sem=sems[1],
+            device_id=partners[i], device_id_type=MESH,
         )
         return copy, exists[i], exists[REVERSE[i]]
 
-    def of_kind(step, *kinds):
-        sizes = {"x": 2, "xy": 4, "xz": 2, "y0": 2, "y1": 2, "z0": 1, "z1": 1, "yz0": 2, "yz1": 2}
-        return [message(step, kind, e) for kind in kinds for e in range(sizes[kind])]
-
-    def start(step, *kinds):
-        for copy, there, _ in of_kind(step, *kinds):
+    def x_messages(step):
+        n = count(step)
+        refs = [(face_x.at[step, d, pl.ds(0, n)], got_x.at[step, d, pl.ds(0, n)], d) for d in range(2)]
+        refs += [(edge_xy.at[step, e], got_xy.at[step, e], 5 + e) for e in range(4)]
+        refs += [(edge_xz.at[step, e], got_xz.at[step, e], 11 + e) for e in range(2)]
+        return [
+            remote(src, dst, (x_send.at[step, k], x_recv.at[step, k]), i)
+            for k, (src, dst, i) in enumerate(refs)
+        ]
+
+    def pair_messages(step, c):
+        refs = [(face_y.at[step, c, d], got_y.at[step, c, d], 2 + d) for d in range(2)]
+        refs += [(edge_yz.at[step, c, d], got_yz.at[step, c, d], 9 + d) for d in range(2)]
+        refs += [(face_z.at[step, c], got_z.at[step, c], 4)]
+        return [
+            remote(src, dst, (pair_send.at[step, c, k], pair_recv.at[step, c, k]), i)
+            for k, (src, dst, i) in enumerate(refs)
+        ]
+
+    def start(copies):
+        for copy, there, _ in copies:
             when(there, copy.start)
 
-    def arrive(step, *kinds):
-        for copy, _, there in of_kind(step, *kinds):
+    def arrive(copies):
+        for copy, _, there in copies:
             when(there, copy.wait_recv)
+
+    def outside_or(condition, value):
+        return jnp.where(condition, jnp.full_like(value, 2.0), value)
+
+    def pack_plane(ext, step, c, side, a):
+        n = count(step)
+        for d, pops in ((0, UP_Y), (1, DOWN_Y)):
+            row = 23 if d == 0 else 8
+            for j, p in enumerate((pops + (MARK,))[:n]):
+                face_y[step, c, d, side, j:j + 1, :] = ext[p, a + 1, row:row + 1, :]
+        for h in range(2):
+            column = jnp.zeros((8, 128), F32)
+            for j in range(n):
+                value = ext[sent_z[j], a + 1, 8 + 8 * h:16 + 8 * h, :]
+                column = jnp.where(flat_lane == j, roll(value, edge_shift[j]), column)
+            face_z[step, c, side, 8 * h:8 * h + 8, :] = column
+            if h == 0:
+                edge_yz[step, c, 1, side, 0:1, :] = column[0:1]
+            else:
+                edge_yz[step, c, 0, side, 0:1, :] = column[7:8]
+
+    def take_pair(ext, step, c):
+        n = count(step)
+        arrive(pair_messages(step, c))
+        for side in range(2):
+            a = plane_of(c, side)
+            for d, pops, row in ((0, UP_Y, 7), (1, DOWN_Y, 24)):
+                outside = (cy == 0) if d == 0 else (cy == n_y - 1)
+                for j, p in enumerate((pops + (MARK,))[:n]):
+                    value = got_y[step, c, d, side, j:j + 1, :]
+                    if p == MARK:
+                        value = outside_or(outside, value)
+                    ext[p, a + 1, row:row + 1, :] = value
+                value = got_yz[step, c, d, side, 0:1, :]
+                if step == 0:
+                    value = jnp.where(flat_lane[0:1] == 5, outside_or(outside, value), value)
+                zext[step, a + 1, row:row + 1, :] = value
+            for h in range(2):
+                zext[step, a + 1, 8 + 8 * h:16 + 8 * h, :] = got_z[
+                    step, c, side, 8 * h:8 * h + 8, :]
 
     def send_x(ext, step):
         n = count(step)
@@ -261,122 +287,35 @@
                 for h in range(2):
                     face_x[step, d, j, 8 * h:8 * h + 8, :] = roll(
                         ext[p, plane, 8 + 8 * h:16 + 8 * h, :], 64)
+            for h in range(2):
+                edge_xz[step, d, 8 * h:8 * h + 8, :] = roll(
+                    face_z[step, 0, 1 - d, 8 * h:8 * h + 8, :], 64)
         for e, (d, j, row) in enumerate(((0, 1, 15), (1, 1, 0), (0, 2, 0), (1, 2, 15))):
             edge_xy[step, e, 0:1, :] = face_x[step, d, j, row:row + 1, :]
             if step == 0:
                 edge_xy[step, e, 1:2, :] = face_x[step, d, 5, row:row + 1, :]
-        for e, (j, plane) in enumerate(((1, 16), (2, 1))):
-            shift = (64 - z_edge) if e == 0 else (128 + 81 - z_edge) % 128
+        start(x_messages(step))
+
+    def take_x(ext, step):
+        n = count(step)
+        arrive(x_messages(step))
+        for d, pops in ((0, UP_X), (1, DOWN_X)):
+            plane, behind = (0, 16) if d == 0 else (17, 1)
+            beyond = low_half if d == 0 else jnp.logical_not(low_half)
+            outside = (s == 0) if d == 0 else (s == n_s - 1)
             for h in range(2):
                 rows = slice(8 + 8 * h, 16 + 8 * h)
-                value = roll(ext[sent_z[j], plane, rows, :], shift)
-                if step == 0:
-                    marks = roll(roll(ext[MARK, plane, rows, :], shift), 1)
-                    value = jnp.where(lane == (0 if e == 0 else 81), value, marks)
-                edge_xz[step, e, 8 * h:8 * h + 8, :] = value
-        start(step, "x", "xy", "xz")
-
-    def send_yz(ext, step, late):
-        n = count(step)
-        flat = ext.reshape(20, 18 * 32, 128)
-        first, planes = late_planes(step)
-        for d, pops in ((0, UP_Y), (1, DOWN_Y)):
-            row = 23 if d == 0 else 8
-            for j, p in enumerate((pops + (MARK,))[:n]):
-                if late:
-                    late_y[step, d, j * planes:(j + 1) * planes, :] = flat[
-                        p, pl.ds(32 * (1 + first) + row, planes, stride=32), :]
-                else:
-                    for h in range(2):
-                        face_y[step, d, j, 8 * h:8 * h + 8, :] = flat[
-                            p, pl.ds(32 * (1 + 8 * h) + row, 8, stride=32), :]
-        start(step, "y1" if late else "y0")
-
-        def gather(i, totals):
-            a = first + i if late else i + (i // first) * planes
-            shift = lax.rem(a + 1 - z_edge + 128, 128)
-            keep = flat_lane == a + 1
-            return tuple(
-                jnp.where(keep, roll(ext[sent_z[j], a + 1, 8 + 8 * h:16 + 8 * h, :], shift),
-                          totals[2 * j + h])
-                for j in range(n) for h in range(2)
-            )
-
-        zero = jnp.zeros((8, 128), F32)
-        totals = lax.fori_loop(0, planes if late else 2 * first, gather, (zero,) * (2 * n))
-        for j in range(n):
-            for h in range(2):
-                face_z[step, late, j, 8 * h:8 * h + 8, :] = totals[2 * j + h]
-        for e, (j, row) in enumerate(((3, 15), (4, 0))):
-            edge_yz[step, late, e, 0:1, :] = face_z[step, late, j, row:row + 1, :]
-            if step == 0:
-                edge_yz[step, late, e, 1:2, :] = face_z[step, late, 5, row:row + 1, :]
-        start(step, "yz1" if late else "yz0", "z1" if late else "z0")
-
-    def outside_or(condition, value):
-        return jnp.where(condition, jnp.full_like(value, 2.0), value)
-
-    def take_yz(ext, step, late):
-        n = count(step)
-        flat = ext.reshape(20, 18 * 32, 128)
-        first, planes = late_planes(step)
-        if late:
-            arrive(step, "z1", "y1", "yz1")
-        else:
-            arrive(step, "z0", "y0", "yz0")
-        for d, pops, row in ((0, UP_Y, 7), (1, DOWN_Y, 24)):
-            outside = (cy == 0) if d == 0 else (cy == n_y - 1)
-            for j, p in enumerate((pops + (MARK,))[:n]):
-                if late:
-                    value = got_late_y[step, d, j * planes:(j + 1) * planes, :]
-                    if p == MARK:
-                        value = outside_or(outside, value)
-                    flat[p, pl.ds(32 * (1 + first) + row, planes, stride=32), :] = value
-                else:
-                    for h in range(2):
-                        value = got_y[step, d, j, 8 * h:8 * h + 8, :]
-                        if p == MARK:
-                            value = outside_or(outside, value)
-                        flat[p, pl.ds(32 * (1 + 8 * h) + row, 8, stride=32), :] = value
-        fresh = (flat_lane > first) & (flat_lane <= first + planes)
-
-        def merge(j, rows, value):
-            if late:
-                value = jnp.where(fresh[0:value.shape[0]], value, zext[step, j, rows, :])
-            zext[step, j, rows, :] = value
-
-        for j in range(n):
-            for h in range(2):
-                value = got_z[step, late, j, 8 * h:8 * h + 8, :]
-                if not late:
-                    fixed = value
-                    if j in (1, 5):
-                        fixed = jnp.where(lane == 64, roll(value, 48), fixed)
-                    if j in (2, 5):
-                        fixed = jnp.where(lane == 17, roll(value, 80), fixed)
-                    value = fixed
-                merge(j, slice(8 + 8 * h, 16 + 8 * h), value)
-        merge(3, slice(7, 8), got_yz[step, late, 0, 0:1, :])
-        merge(4, slice(24, 25), got_yz[step, late, 1, 0:1, :])
-        if step == 0:
-            for e, row in ((0, 7), (1, 24)):
-                outside = (cy == 0) if e == 0 else (cy == n_y - 1)
-                merge(5, slice(row, row + 1), outside_or(outside, got_yz[step, late, e, 1:2, :]))
-
-    def take_x(ext, step):
-        n = count(step)
-        arrive(step, "x", "xy", "xz")
-        for d, pops in ((0, UP_X), (1, DOWN_X)):
-            plane = 0 if d == 0 else 17
-            beyond = low_half if d == 0 else jnp.logical_not(low_half)
-            outside = (s == 0) if d == 0 else (s == n_s - 1)
-            for j, p in enumerate((pops + (MARK,))[:n]):
-                for h in range(2):
+                for j, p in enumerate((pops + (MARK,))[:n]):
                     value = got_x[step, d, j, 8 * h:8 * h + 8, :]
                     if p == MARK:
                         value = outside_or(outside, value)
-                    ext[p, plane, 8 + 8 * h:16 + 8 * h, :] = jnp.where(
+                    ext[p, plane, rows, :] = jnp.where(
                         beyond, value, face_x[step, d, j, 8 * h:8 * h + 8, :])
+                value = got_xz[step, d, 8 * h:8 * h + 8, :]
+                if step == 0:
+                    value = jnp.where(flat_lane == 5, outside_or(outside, value), value)
+                zext[step, plane, rows, :] = jnp.where(
+                    beyond, value, roll(zext[step, behind, rows, :], 64))
         for e, (d, p, row) in enumerate(((0, 7, 7), (1, 8, 24), (0, 9, 24), (1, 10, 7))):
             plane, behind = (0, 16) if d == 0 else (17, 1)
             beyond = (low_half if d == 0 else jnp.logical_not(low_half))[0:1]
@@ -388,17 +327,8 @@
                 value = outside_or(out_x | out_y, got_xy[step, e, 1:2, :])
                 own = roll(ext[MARK, behind, row:row + 1, :], 64)
                 ext[MARK, plane, row:row + 1, :] = jnp.where(beyond, value, own)
-        for e, (j, at) in enumerate(((1, 0), (2, 81))):
-            outside = (s == 0) if e == 0 else (s == n_s - 1)
-            for h in range(2):
-                rows = slice(8 + 8 * h, 16 + 8 * h)
-                value = got_xz[step, e, 8 * h:8 * h + 8, :]
-                zext[step, j, rows, :] = jnp.where(lane == at, value, zext[step, j, rows, :])
-                if step == 0:
-                    marks = outside_or(outside, roll(value, -1))
-                    zext[step, 5, rows, :] = jnp.where(lane == at, marks, zext[step, 5, rows, :])
-
-    def settle(c, carry):
+
+    def settle(c):
         for d in range(2):
             when(exists[1 - d], lambda d=d: move(d, c).wait_recv())
 
@@ -430,13 +360,10 @@
                     ext1[p, a + 1, 8 + 8 * h:16 + 8 * h, :] = post[p]
                 ext1[MARK, a + 1, 8 + 8 * h:16 + 8 * h, :] = marks
                 rho[a, 8 * h:8 * h + 8, :] = density
-
+            pack_plane(ext1, 0, c, side, a)
+
+        start(pair_messages(0, c))
         pl.when(c == 0)(lambda: send_x(ext1, 0))
-        pl.when(c == OUTER - 1)(lambda: send_yz(ext1, 0, 0))
-        return carry
-
-    lax.fori_loop(0, CHUNKS, settle, 0)
-    send_yz(ext1, 0, 1)
 
     first_z = flat_lane == 0
     last_z = flat_lane == 63
@@ -446,9 +373,10 @@
         start_row = 8 + 8 * h - step_y
         return slice(start_row, start_row + 8)
 
+    halo_shift = [lax.rem(128 + z_target - j, 128) for j in range(6)]
+
     def z_halo(step, j, a, h, step_x, step_y):
-        shift = lax.rem(z_target - a + (127 + step_x), 128)
-        return roll(zext[step, j, rows(h, step_y), :], shift)
+        return roll(zext[step, a + 1 - step_x, rows(h, step_y), :], halo_shift[j])
 
     def make_bits(a, h):
         wall = jnp.zeros((8, 128), jnp.int32)
@@ -513,59 +441,77 @@
             settle_one(p, ext[p, a + 1 - step_x, rows(h, step_y), :])
         return new, solid
 
-    take_yz(ext1, 0, 0)
-    take_x(ext1, 0)
-
-    def middle(i, carry):
-        @pl.when(i == 2)
+    def middle(c):
+        @pl.when(c == 0)
         def _():
-            send_x(ext2, 1)
-
-        @pl.when(i == 2 * (OUTER - 1))
+            take_pair(ext1, 0, 0)
+            take_x(ext1, 0)
+
+        pl.when(c < CHUNKS - 1)(lambda: take_pair(ext1, 0, c + 1))
+
+        @pl.loop(0, 2)
+        def _(side):
+            a = plane_of(c, side)
+            for h in range(2):
+                wall, rotor = make_bits(a, h)
+                new, solid = pull(ext1, 0, a, h, wall, rotor)
+                post, density = collide(new, solid)
+                for p in range(19):
+                    ext2[p, a + 1, 8 + 8 * h:16 + 8 * h, :] = post[p]
+                rho[a, 8 * h:8 * h + 8, :] = density
+            pack_plane(ext2, 1, c, side, a)
+
+        start(pair_messages(1, c))
+        pl.when(c == 0)(lambda: send_x(ext2, 1))
+
+    def last(c):
+        @pl.when(c == 0)
         def _():
-            send_yz(ext2, 1, 0)
-            take_yz(ext1, 0, 1)
-
-        a = plane_of(i // 2, i % 2)
-        for h in range(2):
-            wall, rotor = make_bits(a, h)
-            new, solid = pull(ext1, 0, a, h, wall, rotor)
-            post, density = collide(new, solid)
-            for p in range(19):
-                ext2[p, a + 1, 8 + 8 * h:16 + 8 * h, :] = post[p]
-            rho[a, 8 * h:8 * h + 8, :] = density
+            take_pair(ext2, 1, 0)
+            take_x(ext2, 1)
+
+        pl.when(c < CHUNKS - 1)(lambda: take_pair(ext2, 1, c + 1))
+
+        @pl.loop(0, 2)
+        def _(side):
+            a = plane_of(c, side)
+            for h in range(2):
+                wall = walls[a, 8 * h:8 * h + 8, :]
+                rotor = rotors[a, 8 * h:8 * h + 8, :]
+                new, _ = pull(ext2, 1, a, h, wall, rotor)
+                for p in range(19):
+                    out[p, a, 8 * h:8 * h + 8, :] = new[p][:, 0:64]
+                    out[p, EDGE + a, 8 * h:8 * h + 8, :] = roll(new[p], 64)[:, 0:64]
+
+    def collided(t):
+        return jnp.where(t >= 9, 8, jnp.clip(t - 2, 0, 6))
+
+    def streamed(t):
+        return jnp.where(t >= 10, 8, jnp.clip(t - 5, 0, 4))
+
+    def tick(t, carry):
+        @pl.loop(streamed(t - 1), streamed(t))
+        def _(c):
+            last(c)
+
+        pl.when(t < CHUNKS)(lambda: settle(t))
+
+        @pl.loop(collided(t - 1), collided(t))
+        def _(c):
+            middle(c)
+
         return carry
 
-    lax.fori_loop(0, EDGE, middle, 0)
-    send_yz(ext2, 1, 1)
-    take_yz(ext2, 1, 0)
-
-    def last(i, carry):
-        @pl.when(i == 2 * (OUTER - 3))
-        def _():
-            take_yz(ext2, 1, 1)
-
-        @pl.when(i == 14)
-        def _():
-            take_x(ext2, 1)
-
-        a = plane_of((i // 2 + 1) % 8, i % 2)
-        for h in range(2):
-            wall = walls[a, 8 * h:8 * h + 8, :]
-            rotor = rotors[a, 8 * h:8 * h + 8, :]
-            new, _ = pull(ext2, 1, a, h, wall, rotor)
-            for p in range(19):
-                out[p, a, 8 * h:8 * h + 8, :] = new[p][:, 0:64]
-                out[p, EDGE + a, 8 * h:8 * h + 8, :] = roll(new[p], 64)[:, 0:64]
-        return carry
-
-    lax.fori_loop(0, EDGE, last, 0)
+    lax.fori_loop(0, 11, tick, 0)
     for c in range(CHUNKS):
         for d in range(2):
             when(exists[d], lambda d=d, c=c: move(d, c).wait_send())
     for step in range(2):
-        for copy, there, _ in of_kind(step, "x", "xy", "xz", "y0", "y1", "z0", "z1", "yz0", "yz1"):
+        for copy, there, _ in x_messages(step):
             when(there, copy.wait_send)
+        for c in range(CHUNKS):
+            for copy, there, _ in pair_messages(step, c):
+                when(there, copy.wait_send)
 
 
 def step_all(populations, solid_cells, block_pos):
@@ -586,20 +532,21 @@
     for _ in range(2):
         scratch += [
             pltpu.VMEM((2, 2, 6, 16, 128), F32),
-            pltpu.VMEM((2, 2, 6, 16, 128), F32),
-            pltpu.VMEM((2, 2, 48, 128), F32),
-            pltpu.VMEM((2, 2, 6, 16, 128), F32),
+            pltpu.VMEM((2, CHUNKS, 2, 2, 8, 128), F32),
+            pltpu.VMEM((2, CHUNKS, 2, 16, 128), F32),
             pltpu.VMEM((2, 4, 8, 128), F32),
-            pltpu.VMEM((2, 2, 2, 8, 128), F32),
+            pltpu.VMEM((2, CHUNKS, 2, 2, 8, 128), F32),
             pltpu.VMEM((2, 2, 16, 128), F32),
         ]
     scratch += [
-        pltpu.VMEM((2, 6, 32, 128), F32),
+        pltpu.VMEM((2, 18, 32, 128), F32),
         pltpu.SemaphoreType.DMA((6,)),
         pltpu.SemaphoreType.DMA((2, CHUNKS)),
         pltpu.SemaphoreType.DMA((2, CHUNKS)),
-        pltpu.SemaphoreType.DMA((2, 18)),
-        pltpu.SemaphoreType.DMA((2, 18)),
+        pltpu.SemaphoreType.DMA((2, 8)),
+        pltpu.SemaphoreType.DMA((2, 8)),
+        pltpu.SemaphoreType.DMA((2, CHUNKS, 5)),
+        pltpu.SemaphoreType.DMA((2, CHUNKS, 5)),
     ]
     return pl.pallas_call(
         kernel,

time: 39.1 us -> 46.2 us (1.18)
  Pallas kernels: 36.7 us -> 43.9 us
    pallas_call x1, Pallas kernels: 36.7 us -> 43.9 us  [step_all(): pl.pallas_call(kernel, out_shape=jax.ShapeDtypeStruct((19, 32, 16, 64), F...]
where the time goes in v3:
time: 46.2 us; the launch traced here: 46.1 us
  Pallas kernels  43.9 us (95%)
  local copies, waits for them, and re-layouts  2.27 us (5%)
    pallas_call x1, Pallas kernels, step_all(): pl.pallas_call(kernel, out_shape=jax.ShapeDtypeStruct((19, 32, 16, 64), F...  43.9 us
    unnamed x1, local copies, waits for them, and re-layouts  2.27 us

profile of v3, /device:TPU:7, one launch (start us, length us, event | category | flops | bytes accessed | tf_op | source)
XLA Modules:
  0.0 46.1 jit_solution(9560734350498779493)
XLA Ops:
  0.0 43.9 %shard_map.37 = f32[19,32,16,64]{3,2,1,0:T(8,128)S(1)} custom-call(s32[3,12]{1,0:T(4,128)} %bitcast.1, f32[12,19,4096]{2,1,0:T(8,128)} %pop_in.1, s32[12,4096]{1,0:T(8,128)} %mark_in.1), custom_call_target="tpu_custom_call" | custom-call | tf_op jit(solution)/shard_map/pallas_call | solution.py:551
  43.9 2.3 %copy.5 = f32[19,32,16,64]{3,2,1,0:T(8,128)} copy(f32[19,32,16,64]{3,2,1,0:T(8,128)S(1)} %shard_map.37) | data formatting | bytes 4980736

commit v4 on v3

--- a/solution.py
+++ b/solution.py
@@ -213,8 +213,7 @@
         return copy, exists[i], exists[REVERSE[i]]
 
     def x_messages(step):
-        n = count(step)
-        refs = [(face_x.at[step, d, pl.ds(0, n)], got_x.at[step, d, pl.ds(0, n)], d) for d in range(2)]
+        refs = [(face_x.at[step, d], got_x.at[step, d], d) for d in range(2)]
         refs += [(edge_xy.at[step, e], got_xy.at[step, e], 5 + e) for e in range(4)]
         refs += [(edge_xz.at[step, e], got_xz.at[step, e], 11 + e) for e in range(2)]
         return [
@@ -283,17 +282,22 @@
         n = count(step)
         for d, pops in ((0, UP_X), (1, DOWN_X)):
             plane = 16 if d == 0 else 1
-            for j, p in enumerate((pops + (MARK,))[:n]):
-                for h in range(2):
-                    face_x[step, d, j, 8 * h:8 * h + 8, :] = roll(
-                        ext[p, plane, 8 + 8 * h:16 + 8 * h, :], 64)
+            beyond = low_half if d == 0 else jnp.logical_not(low_half)
             for h in range(2):
+                values = [
+                    ext[p, plane, 8 + 8 * h:16 + 8 * h, :] for p in (pops + (MARK,))[:n]
+                ]
+                for j in range(0, n, 2):
+                    value = roll(values[j], 64)
+                    if j + 1 < n:
+                        value = jnp.where(beyond, value, values[j + 1])
+                    face_x[step, d, j // 2, 8 * h:8 * h + 8, :] = value
                 edge_xz[step, d, 8 * h:8 * h + 8, :] = roll(
                     face_z[step, 0, 1 - d, 8 * h:8 * h + 8, :], 64)
-        for e, (d, j, row) in enumerate(((0, 1, 15), (1, 1, 0), (0, 2, 0), (1, 2, 15))):
-            edge_xy[step, e, 0:1, :] = face_x[step, d, j, row:row + 1, :]
+        for e, (plane, p, row) in enumerate(((16, 7, 23), (1, 8, 8), (16, 9, 8), (1, 10, 23))):
+            edge_xy[step, e, 0:1, :] = roll(ext[p, plane, row:row + 1, :], 64)
             if step == 0:
-                edge_xy[step, e, 1:2, :] = face_x[step, d, 5, row:row + 1, :]
+                edge_xy[step, e, 1:2, :] = roll(ext[MARK, plane, row:row + 1, :], 64)
         start(x_messages(step))
 
     def take_x(ext, step):
@@ -306,11 +310,12 @@
             for h in range(2):
                 rows = slice(8 + 8 * h, 16 + 8 * h)
                 for j, p in enumerate((pops + (MARK,))[:n]):
-                    value = got_x[step, d, j, 8 * h:8 * h + 8, :]
+                    value = got_x[step, d, j // 2, 8 * h:8 * h + 8, :]
+                    if j % 2:
+                        value = roll(value, 64)
                     if p == MARK:
                         value = outside_or(outside, value)
-                    ext[p, plane, rows, :] = jnp.where(
-                        beyond, value, face_x[step, d, j, 8 * h:8 * h + 8, :])
+                    ext[p, plane, rows, :] = jnp.where(beyond, value, roll(ext[p, behind, rows, :], 64))
                 value = got_xz[step, d, 8 * h:8 * h + 8, :]
                 if step == 0:
                     value = jnp.where(flat_lane == 5, outside_or(outside, value), value)
@@ -441,13 +446,16 @@
             settle_one(p, ext[p, a + 1 - step_x, rows(h, step_y), :])
         return new, solid
 
-    def middle(c):
-        @pl.when(c == 0)
-        def _():
-            take_pair(ext1, 0, 0)
-            take_x(ext1, 0)
-
-        pl.when(c < CHUNKS - 1)(lambda: take_pair(ext1, 0, c + 1))
+    def middle(p):
+        def taken(p):
+            return jnp.where(p < 0, 0, jnp.where(p < 4, p + 3, jnp.minimum(p + 2, 8)))
+
+        @pl.loop(taken(p - 1), taken(p))
+        def _(c):
+            take_pair(ext1, 0, c)
+
+        pl.when(p == 4)(lambda: take_x(ext1, 0))
+        c = jnp.where(p < 4, p + 1, jnp.where(p == 4, 0, p))
 
         @pl.loop(0, 2)
         def _(side):
@@ -462,15 +470,18 @@
             pack_plane(ext2, 1, c, side, a)
 
         start(pair_messages(1, c))
-        pl.when(c == 0)(lambda: send_x(ext2, 1))
-
-    def last(c):
-        @pl.when(c == 0)
-        def _():
-            take_pair(ext2, 1, 0)
-            take_x(ext2, 1)
-
-        pl.when(c < CHUNKS - 1)(lambda: take_pair(ext2, 1, c + 1))
+        pl.when(p == 4)(lambda: send_x(ext2, 1))
+
+    def last(p):
+        def taken(p):
+            return jnp.where(p < 0, 0, jnp.minimum(p + 3, 8))
+
+        @pl.loop(taken(p - 1), taken(p))
+        def _(u):
+            take_pair(ext2, 1, jnp.where(u < 5, u + 1, jnp.where(u == 5, 0, u)))
+
+        pl.when(p == 7)(lambda: take_x(ext2, 1))
+        c = jnp.where(p < 3, p + 2, jnp.where(p == 3, 1, jnp.where(p == 7, 0, p + 1)))
 
         @pl.loop(0, 2)
         def _(side):
@@ -484,10 +495,10 @@
                     out[p, EDGE + a, 8 * h:8 * h + 8, :] = roll(new[p], 64)[:, 0:64]
 
     def collided(t):
-        return jnp.where(t >= 9, 8, jnp.clip(t - 2, 0, 6))
+        return jnp.where(t >= 9, 8, jnp.where(t == 8, 6, jnp.clip(t - 3, 0, 4)))
 
     def streamed(t):
-        return jnp.where(t >= 10, 8, jnp.clip(t - 5, 0, 4))
+        return jnp.where(t >= 10, 8, jnp.where(t == 9, 1, 0))
 
     def tick(t, carry):
         @pl.loop(streamed(t - 1), streamed(t))
@@ -531,7 +542,7 @@
     ]
     for _ in range(2):
         scratch += [
-            pltpu.VMEM((2, 2, 6, 16, 128), F32),
+            pltpu.VMEM((2, 2, 3, 16, 128), F32),
             pltpu.VMEM((2, CHUNKS, 2, 2, 8, 128), F32),
             pltpu.VMEM((2, CHUNKS, 2, 16, 128), F32),
             pltpu.VMEM((2, 4, 8, 128), F32),

time: 46.2 us -> 36.8 us (0.80)
  Pallas kernels: 43.9 us -> 34.4 us
    pallas_call x1, Pallas kernels: 43.9 us -> 34.4 us  [step_all(): pl.pallas_call(kernel, out_shape=jax.ShapeDtypeStruct((19, 32, 16, 64), F...]
where the time goes in v4:
time: 36.8 us; the launch traced here: 36.7 us
  Pallas kernels  34.4 us (93%)
  local copies, waits for them, and re-layouts  2.27 us (6%)
    pallas_call x1, Pallas kernels, step_all(): pl.pallas_call(kernel, out_shape=jax.ShapeDtypeStruct((19, 32, 16, 64), F...  34.4 us
    unnamed x1, local copies, waits for them, and re-layouts  2.27 us

profile of v4, /device:TPU:7, one launch (start us, length us, event | category | flops | bytes accessed | tf_op | source)
XLA Modules:
  0.0 36.7 jit_solution(15379992214291427138)
XLA Ops:
  0.0 34.4 %shard_map.37 = f32[19,32,16,64]{3,2,1,0:T(8,128)S(1)} custom-call(s32[3,12]{1,0:T(4,128)} %bitcast.1, f32[12,19,4096]{2,1,0:T(8,128)} %pop_in.1, s32[12,4096]{1,0:T(8,128)} %mark_in.1), custom_call_target="tpu_custom_call" | custom-call | tf_op jit(solution)/shard_map/pallas_call | solution.py:562
  34.4 2.3 %copy.5 = f32[19,32,16,64]{3,2,1,0:T(8,128)} copy(f32[19,32,16,64]{3,2,1,0:T(8,128)S(1)} %shard_map.37) | data formatting | bytes 4980736

commit v5 on v4

--- a/solution.py
+++ b/solution.py
@@ -23,6 +23,7 @@
 UP_Y = (3, 7, 10, 15, 17)
 DOWN_Y = (4, 8, 9, 16, 18)
 MARK = 19
+ROTOR_CODE = 0x10001
 
 EDGE = 16
 CHUNKS = 8
@@ -58,7 +59,7 @@
         odd = (4.0 / 9.0) * minus[k] - (8.0 / 3.0 * weight) * m
         post[i] = f[i] - even - odd
         post[o] = f[o] - even + odd
-    return [jnp.where(mark, f[i], post[i]) for i in range(19)], density
+    return [jnp.where(mark, f[0], post[0])] + [jnp.where(mark, f[OPPOSITE[i]], post[i]) for i in range(1, 19)], density
 
 
 def group_swap(values):
@@ -78,7 +79,7 @@
 
 
 def kernel(pos_in, pop_in, mark_in, out, held, marks_in, held_marks, pos, send, recv, stage, ext1, ext2,
-           rho, walls, rotors, face_x, face_y, face_z, edge_xy, edge_yz, edge_xz,
+           codes, rho, walls, rotors, face_x, face_y, face_z, edge_xy, edge_yz, edge_xz,
            got_x, got_y, got_z, got_xy, got_yz, got_xz, zext,
            in_sem, move_send, move_recv, x_send, x_recv, pair_send, pair_recv):
     s = lax.axis_index("stream")
@@ -111,7 +112,8 @@
     loads = [pltpu.make_async_copy(pos_in, pos, in_sem.at[0]),
              pltpu.make_async_copy(mark_in, marks_in, in_sem.at[1])]
     loads += [
-        pltpu.make_async_copy(pop_in.at[pl.ds(3 * i, 3)], held.at[pl.ds(3 * i, 3)], in_sem.at[2 + i])
+        pltpu.make_async_copy(
+            pop_in.at[pl.ds(3 * i, 3)], held.at[pl.ds(3 * i, 3), :, pl.ds(0, 4096)], in_sem.at[2 + i])
         for i in range(4)
     ]
     for load in loads:
@@ -149,11 +151,9 @@
         for z in range(4):
             order.append(jnp.minimum(missing, 1))
             missing = missing + jnp.where(source[layer * 4 + z] < 0, 1, 0)
-    here = [jnp.full((8, 128), source[j], jnp.int32) >= 0 for j in range(8)]
-    here4 = [jnp.full((4, 128), source[j], jnp.int32) >= 0 for j in range(8)]
-    later = [jnp.full((8, 128), order[j], jnp.int32) > 0 for j in range(8)]
-    second = [jnp.full((4, 128), order[j], jnp.int32) > 0 for j in range(8)]
-    source = [jnp.maximum(source[j], 0) for j in range(8)]
+    source = [
+        jnp.where(source[j] < 0, ROWS + 2 * (j // 4) + order[j], source[j]) for j in range(8)
+    ]
 
     for load in loads[1:]:
         load.wait()
@@ -240,6 +240,10 @@
 
     def outside_or(condition, value):
         return jnp.where(condition, jnp.full_like(value, 2.0), value)
+
+    def code_or(condition, value):
+        code = jnp.where(value > 0.5, ROTOR_CODE, 0)
+        return jnp.where(condition, jnp.full_like(code, 1), code)
 
     def pack_plane(ext, step, c, side, a):
         n = count(step)
@@ -268,8 +272,9 @@
                 for j, p in enumerate((pops + (MARK,))[:n]):
                     value = got_y[step, c, d, side, j:j + 1, :]
                     if p == MARK:
-                        value = outside_or(outside, value)
-                    ext[p, a + 1, row:row + 1, :] = value
+                        codes[a + 1, row:row + 1, :] = code_or(outside, value)
+                    else:
+                        ext[p, a + 1, row:row + 1, :] = value
                 value = got_yz[step, c, d, side, 0:1, :]
                 if step == 0:
                     value = jnp.where(flat_lane[0:1] == 5, outside_or(outside, value), value)
@@ -314,8 +319,11 @@
                     if j % 2:
                         value = roll(value, 64)
                     if p == MARK:
-                        value = outside_or(outside, value)
-                    ext[p, plane, rows, :] = jnp.where(beyond, value, roll(ext[p, behind, rows, :], 64))
+                        codes[plane, rows, :] = jnp.where(
+                            beyond, code_or(outside, value), roll(codes[behind, rows, :], 64))
+                    else:
+                        ext[p, plane, rows, :] = jnp.where(
+                            beyond, value, roll(ext[p, behind, rows, :], 64))
                 value = got_xz[step, d, 8 * h:8 * h + 8, :]
                 if step == 0:
                     value = jnp.where(flat_lane == 5, outside_or(outside, value), value)
@@ -329,41 +337,47 @@
             if step == 0:
                 out_x = (s == 0) if d == 0 else (s == n_s - 1)
                 out_y = (cy == 0) if row == 7 else (cy == n_y - 1)
-                value = outside_or(out_x | out_y, got_xy[step, e, 1:2, :])
-                own = roll(ext[MARK, behind, row:row + 1, :], 64)
-                ext[MARK, plane, row:row + 1, :] = jnp.where(beyond, value, own)
+                value = code_or(out_x | out_y, got_xy[step, e, 1:2, :])
+                own = roll(codes[behind, row:row + 1, :], 64)
+                codes[plane, row:row + 1, :] = jnp.where(beyond, value, own)
 
     def settle(c):
         for d in range(2):
             when(exists[1 - d], lambda d=d: move(d, c).wait_recv())
+
+        @pl.loop(0, TILES)
+        def _(kk):
+            k = 2 * plane_of(c, kk // 2) + kk % 2
+            for d in range(2):
+                last_rows = recv[d, c, kk, 4]
+                for q in range(2):
+                    row = ROWS + 2 * d + q
+                    held[row, 0:8, cells(k)] = recv[d, c, kk, 2 * q]
+                    held[row, 8:16, cells(k)] = recv[d, c, kk, 2 * q + 1]
+                    held[row, 16:19, cells(k)] = last_rows[4 * q:4 * q + 3]
+                    held_marks[row, :, cells(k)] = last_rows[4 * q + 3:4 * q + 4]
 
         @pl.loop(0, 2)
         def _(side):
             a = plane_of(c, side)
             for h in range(2):
-                kk = side * 2 + h
                 k = 2 * a + h
                 for t in range(3):
-                    tiles = []
-                    for j in range(8):
-                        d = j // 4
-                        if t < 2:
-                            mine = held[source[j], 8 * t:8 * t + 8, cells(k)]
-                            theirs = jnp.where(later[j], recv[d, c, kk, 2 + t], recv[d, c, kk, t])
-                            tiles.append(jnp.where(here[j], mine, theirs))
-                        else:
-                            theirs = recv[d, c, kk, 4]
-                            theirs = jnp.where(second[j], theirs[4:8], theirs[0:4])
-                            tiles.append(jnp.where(here4[j], tail(source[j], k), theirs))
+                    if t < 2:
+                        tiles = [held[source[j], 8 * t:8 * t + 8, cells(k)] for j in range(8)]
+                    else:
+                        tiles = [tail(source[j], k) for j in range(8)]
                     height = tiles[0].shape[0]
                     for g, value in enumerate(group_swap(tiles)):
-                        stage[t, 8 * g:8 * g + height, :] = value
-                f = [stage[p // 8, pl.ds(p % 8, 8, stride=8), :] for p in range(19)]
-                marks = stage[2, pl.ds(3, 8, stride=8), :]
+                        stage[h, t, 9 * g:9 * g + height, :] = value
+            for h in range(2):
+                f = [stage[h, p // 8, pl.ds(p % 8, 8, stride=9), :] for p in range(19)]
+                marks = stage[h, 2, pl.ds(3, 8, stride=9), :]
                 post, density = collide(f, marks > 0.5)
                 for p in range(19):
                     ext1[p, a + 1, 8 + 8 * h:16 + 8 * h, :] = post[p]
                 ext1[MARK, a + 1, 8 + 8 * h:16 + 8 * h, :] = marks
+                codes[a + 1, 8 + 8 * h:16 + 8 * h, :] = jnp.where(marks > 0.5, ROTOR_CODE, 0)
                 rho[a, 8 * h:8 * h + 8, :] = density
             pack_plane(ext1, 0, c, side, a)
 
@@ -384,32 +398,38 @@
         return roll(zext[step, a + 1 - step_x, rows(h, step_y), :], halo_shift[j])
 
     def make_bits(a, h):
-        wall = jnp.zeros((8, 128), jnp.int32)
-        rotor = jnp.zeros((8, 128), jnp.int32)
-
-        def add(bit, value):
-            nonlocal wall, rotor
-            wall = wall + jnp.where(value > 0.5, 1 << bit, 0)
-            if bit > 2:
-                rotor = rotor + jnp.where(value == 1.0, 1 << bit, 0)
-
+        words = [jnp.zeros((8, 128), jnp.int32)] * 2
+
+        def add(p, code):
+            words[p // 16] = words[p // 16] | (code << (p - 15 * (p // 16)))
+
+        solid = None
         for step_x, step_y, p_flat, p_up, p_down in GROUPS:
-            value = ext1[MARK, a + 1 - step_x, rows(h, step_y), :]
-            add(p_flat, value)
+            code = codes[a + 1 - step_x, rows(h, step_y), :]
+            if p_flat:
+                add(p_flat, code)
+            else:
+                solid = code != 0
             halo = z_halo(0, 5, a, h, step_x, step_y)
-            add(p_up, jnp.where(first_z, outside_or(core == 0, halo), roll(value, 1)))
-            add(p_down, jnp.where(last_z, outside_or(core == 1, halo), roll(value, -1)))
+            halo = jnp.where(halo > 1.5, 1, jnp.where(halo > 0.5, ROTOR_CODE, 0))
+            wall = jnp.full_like(code, 1)
+            add(p_up, jnp.where(first_z, jnp.where(core == 0, wall, halo), roll(code, 1)))
+            add(p_down, jnp.where(last_z, jnp.where(core == 1, wall, halo), roll(code, -1)))
         for step_x, step_y, p in DIAGONALS:
-            add(p, ext1[MARK, a + 1 - step_x, rows(h, step_y), :])
-        walls[a, 8 * h:8 * h + 8, :] = wall
-        rotors[a, 8 * h:8 * h + 8, :] = rotor
-        return wall, rotor
+            add(p, codes[a + 1 - step_x, rows(h, step_y), :])
+        walls[a, 8 * h:8 * h + 8, :] = jnp.where(solid, 0xFFFF, words[0])
+        rotors[a, 8 * h:8 * h + 8, :] = jnp.where(solid, 0xE, words[1])
+        return walls[a, 8 * h:8 * h + 8, :], rotors[a, 8 * h:8 * h + 8, :]
+
+    def bit(words, p, base):
+        at = base + p - 15 * (p // 16)
+        return (words[p // 16] & (-(1 << 31) if at == 31 else 1 << at)) != 0
 
     along_z = (core * 64 + flat_lane).astype(F32) - 63.5
     drift_a = (-OMEGA / 6.0) * along_z
     sub = lax.broadcasted_iota(jnp.int32, (8, 128), 0)
 
-    def pull(ext, step, a, h, wall, rotor):
+    def pull(ext, step, a, h, words):
         here_rows = slice(8 + 8 * h, 16 + 8 * h)
         centre = [ext[p, a + 1, here_rows, :] for p in range(19)]
         density = rho[a, 8 * h:8 * h + 8, :]
@@ -423,16 +443,15 @@
             11: push_b, 12: -push_b, 13: -push_b, 14: push_b,
             15: both, 16: -both, 17: apart, 18: -apart,
         }
-        solid = (wall & 1) != 0
+        solid = bit(words, 0, 0)
         new = [None] * 19
         new[0] = centre[0]
 
         def settle_one(p, pulled):
             bounced = centre[OPPOSITE[p]]
             if p > 2:
-                bounced = bounced + jnp.where((rotor & (1 << p)) != 0, push[p], 0.0)
-            value = jnp.where((wall & (1 << p)) != 0, bounced, pulled)
-            new[p] = jnp.where(solid, centre[p], value)
+                bounced = bounced + jnp.where(bit(words, p, 16), push[p], 0.0)
+            new[p] = jnp.where(bit(words, p, 0), bounced, pulled)
 
         for j, (step_x, step_y, p_flat, p_up, p_down) in enumerate(GROUPS):
             if p_flat:
@@ -461,8 +480,7 @@
         def _(side):
             a = plane_of(c, side)
             for h in range(2):
-                wall, rotor = make_bits(a, h)
-                new, solid = pull(ext1, 0, a, h, wall, rotor)
+                new, solid = pull(ext1, 0, a, h, make_bits(a, h))
                 post, density = collide(new, solid)
                 for p in range(19):
                     ext2[p, a + 1, 8 + 8 * h:16 + 8 * h, :] = post[p]
@@ -487,9 +505,8 @@
         def _(side):
             a = plane_of(c, side)
             for h in range(2):
-                wall = walls[a, 8 * h:8 * h + 8, :]
-                rotor = rotors[a, 8 * h:8 * h + 8, :]
-                new, _ = pull(ext2, 1, a, h, wall, rotor)
+                words = (walls[a, 8 * h:8 * h + 8, :], rotors[a, 8 * h:8 * h + 8, :])
+                new, _ = pull(ext2, 1, a, h, words)
                 for p in range(19):
                     out[p, a, 8 * h:8 * h + 8, :] = new[p][:, 0:64]
                     out[p, EDGE + a, 8 * h:8 * h + 8, :] = roll(new[p], 64)[:, 0:64]
@@ -498,7 +515,7 @@
         return jnp.where(t >= 9, 8, jnp.where(t == 8, 6, jnp.clip(t - 3, 0, 4)))
 
     def streamed(t):
-        return jnp.where(t >= 10, 8, jnp.where(t == 9, 1, 0))
+        return jnp.where(t >= 10, 8, 0)
 
     def tick(t, carry):
         @pl.loop(streamed(t - 1), streamed(t))
@@ -527,15 +544,16 @@
 
 def step_all(populations, solid_cells, block_pos):
     scratch = [
-        pltpu.VMEM((ROWS, 19, 4096), F32),
+        pltpu.VMEM((ROWS + 4, 19, 4224), F32),
         pltpu.VMEM((ROWS, 4096), jnp.int32),
-        pltpu.VMEM((ROWS, 1, 4096), F32),
+        pltpu.VMEM((ROWS + 5, 1, 4096), F32),
         pltpu.SMEM((3, ROWS), jnp.int32),
         pltpu.VMEM((2, CHUNKS, TILES, 5, 8, 128), F32),
         pltpu.VMEM((2, CHUNKS, TILES, 5, 8, 128), F32),
-        pltpu.VMEM((3, 64, 128), F32),
-        pltpu.VMEM((20, 18, 32, 128), F32),
-        pltpu.VMEM((20, 18, 32, 128), F32),
+        pltpu.VMEM((2, 3, 88, 128), F32),
+        pltpu.VMEM((20, 19, 40, 128), F32),
+        pltpu.VMEM((20, 19, 40, 128), F32),
+        pltpu.VMEM((18, 32, 128), jnp.int32),
         pltpu.VMEM((EDGE, 16, 128), F32),
         pltpu.VMEM((EDGE, 16, 128), jnp.int32),
         pltpu.VMEM((EDGE, 16, 128), jnp.int32),
@@ -543,10 +561,10 @@
     for _ in range(2):
         scratch += [
             pltpu.VMEM((2, 2, 3, 16, 128), F32),
-            pltpu.VMEM((2, CHUNKS, 2, 2, 8, 128), F32),
+            pltpu.VMEM((2, CHUNKS + 1, 2, 2, 8, 128), F32),
             pltpu.VMEM((2, CHUNKS, 2, 16, 128), F32),
             pltpu.VMEM((2, 4, 8, 128), F32),
-            pltpu.VMEM((2, CHUNKS, 2, 2, 8, 128), F32),
+            pltpu.VMEM((2, CHUNKS + 1, 2, 2, 8, 128), F32),
             pltpu.VMEM((2, 2, 16, 128), F32),
         ]
     scratch += [
@@ -566,7 +584,7 @@
         out_specs=pl.BlockSpec(memory_space=pltpu.VMEM),
         scratch_shapes=scratch,
         compiler_params=pltpu.CompilerParams(
-            collective_id=0, has_side_effects=True, vmem_limit_bytes=40 * 1024 * 1024
+            collective_id=0, has_side_effects=True, vmem_limit_bytes=44 * 1024 * 1024
         ),
     )(*(pltpu.with_memory_space_constraint(value, pltpu.HBM)
         for value in (block_pos.T, populations, solid_cells)))

time: 36.8 us -> 36.8 us (level)
  no operation moved by 1% of the time
where the time goes in v5:
time: 36.8 us; the launch traced here: 36.7 us
  Pallas kernels  34.4 us (93%)
  local copies, waits for them, and re-layouts  2.27 us (6%)
    pallas_call x1, Pallas kernels, step_all(): pl.pallas_call(kernel, out_shape=jax.ShapeDtypeStruct((19, 32, 16, 64), F...  34.4 us
    unnamed x1, local copies, waits for them, and re-layouts  2.27 us

profile of v5, /device:TPU:7, one launch (start us, length us, event | category | flops | bytes accessed | tf_op | source)
XLA Modules:
  0.0 36.7 jit_solution(11186463973292497107)
XLA Ops:
  0.0 34.4 %shard_map.37 = f32[19,32,16,64]{3,2,1,0:T(8,128)S(1)} custom-call(s32[3,12]{1,0:T(4,128)} %bitcast.1, f32[12,19,4096]{2,1,0:T(8,128)} %pop_in.1, s32[12,4096]{1,0:T(8,128)} %mark_in.1), custom_call_target="tpu_custom_call" | custom-call | tf_op jit(solution)/shard_map/pallas_call | solution.py:580
  34.4 2.3 %copy.5 = f32[19,32,16,64]{3,2,1,0:T(8,128)} copy(f32[19,32,16,64]{3,2,1,0:T(8,128)S(1)} %shard_map.37) | data formatting | bytes 4980736
